TPU v7x, 512 devices: a whole 4x8x8 slice. The times are simulated.
512 devices in a mesh: tm: 16 (over y, z_lo), slab: 32 (over x, z_hi, core).
Axes of the slice: x: 4, y: 8, z: 8 (z_hi: 4, z_lo: 2; z = z_hi * 2 + z_lo), core: 2. Of those that a mesh axis runs over, the one named last changes fastest.
Arguments:
- velocity: bfloat16 [16, 3, 2, 524288], P('tm', None, None, 'slab'), may hold values from -64 to 64
- shell_index: int32 [524288], P('slab'), may hold values from 0 to 127, as said below
- ref_order: int32 [16], replicated, may hold values from 0 to 15, each once
Outputs:
- coherence: float32 [16, 16, 128], P('tm')
- spectrum: float32 [16, 128], P('tm')
Inputs may be any that keep to these rules, and one draw needn't show every extreme that they name: `shell_index`: every shell number from 0 to 127 is taken by some mode. `ref_order`: each snapshot number appears once.
All inputs are finite; a program needn't handle non-finite values.
Results may differ from a plain program's by a relative error of at most 0.0003.
Values may be sent and summed in bfloat16 or wider, within the bound.
A program may use at most 64 MiB of HBM per device.

v0:
```python
import math

import jax
import jax.numpy as jnp
from jax import lax
from jax.sharding import Mesh
from jax.sharding import PartitionSpec as P

SHELLS = 128
TM = ("tm_0", "tm_1")


def cut_along(array, dim, devices):
    before, after = (array.shape[:dim], array.shape[dim + 1 :])
    return jnp.moveaxis(array.reshape(*before, devices, -1, *after), dim, 0)


def in_order(parts, dim):
    parts = jnp.moveaxis(parts, 0, dim)
    shape = parts.shape
    return parts.reshape(*shape[:dim], shape[dim] * shape[dim + 1], *shape[dim + 2 :])


def turned_blocks(parts, axes, turns):
    inside = parts.shape[1:]
    whole = parts.reshape(*(lax.axis_size(a) for a in axes), *inside)
    for k in turns:
        whole = lax.all_to_all(whole, axes[k], k, k, tiled=True)
    return whole.reshape(-1, *inside)


def stepwise_exchange(array, axes, turns, split_dim, concat_dim):
    parts = cut_along(array, split_dim, lax.axis_size(axes))
    return in_order(turned_blocks(parts, axes, turns), concat_dim)


def sum_at_owner(array, axis, dim):
    devices = lax.axis_size(axis)
    parts = lax.all_to_all(cut_along(array, dim, devices), axis, 0, 0, tiled=True)
    return jnp.sum(parts, axis=0)


def in_one_piece(arrays, axis, dim, along):
    ends, at = ([], 0)
    for a in arrays[:-1]:
        at += a.shape[along]
        ends.append(at)
    both = jnp.concatenate(arrays, axis=along)
    return tuple(jnp.split(sum_at_owner(both, axis, dim), ends, axis=along))


def copy_for_each(array, axis):
    devices = lax.axis_size(axis)
    return lax.all_to_all(
        jnp.broadcast_to(array[None], (devices, *array.shape)), axis, 0, 0, tiled=True
    )


def over_copies(array, axis):
    everything = copy_for_each(array, axis)
    return jnp.sum(everything, axis=0)


def packed_total(arrays, axis):
    vector, at, outs = (jnp.concatenate([a.reshape(-1) for a in arrays]), 0, [])
    so_far = over_copies(vector, axis)
    for a in arrays:
        outs.append(so_far[at : at + a.size].reshape(a.shape))
        at += a.size
    return tuple(outs)


def gathered_copies(array, axis, dim):
    parts = copy_for_each(array, axis)
    return in_order(parts, dim)


def bin_modes(cross_terms, energy_terms, shell_ids):
    mode_count = cross_terms.shape[1]
    block_size = math.gcd(mode_count, 4096)
    columns = jnp.arange(SHELLS, dtype=jnp.int32)

    def add_block(step_index, totals):
        onehot = (shell_ids[:, None] == columns[None, :]).astype(jnp.bfloat16)
        return (
            totals[0] + jnp.dot(cross_terms, onehot, preferred_element_type=jnp.float32),
            totals[1] + jnp.dot(energy_terms, onehot, preferred_element_type=jnp.float32),
        )

    initial = (
        jnp.zeros((cross_terms.shape[0], SHELLS), jnp.float32),
        jnp.zeros((energy_terms.shape[0], SHELLS), jnp.float32),
    )
    return lax.fori_loop(0, mode_count // block_size, add_block, initial)


def body(velocity, shell_index, ref_order):
    snapshots = lax.axis_size(TM)
    mode_count = velocity.shape[3]
    local_modes = stepwise_exchange(velocity, TM, (0, 1), 3, 0)
    part_size = mode_count // snapshots
    shell_ids = lax.dynamic_slice_in_dim(shell_index, lax.axis_index(TM) * part_size, part_size, 0)
    rotated = jnp.stack([local_modes[:, :, 1], -local_modes[:, :, 0]], axis=2)
    real_part = jnp.einsum(
        "tcpm,rcpm->trm", local_modes, local_modes, preferred_element_type=jnp.float32
    )
    imag_part = jnp.einsum(
        "tcpm,rcpm->trm", rotated, local_modes, preferred_element_type=jnp.float32
    )
    cross_terms = jnp.stack([real_part, imag_part], axis=2).astype(jnp.bfloat16)
    cross_terms = cross_terms.reshape(snapshots * snapshots * 2, part_size)
    wide_modes = local_modes.astype(jnp.float32)
    energy_terms = jnp.sum(wide_modes * wide_modes, axis=(1, 2)).astype(jnp.bfloat16)
    cross_binned, energy_binned = bin_modes(cross_terms, energy_terms, shell_ids)
    cross_own, energy_own = in_one_piece(
        (cross_binned.reshape(snapshots, snapshots * 2 * SHELLS), energy_binned), TM, 0, 1
    )
    partial_cross = cross_own.reshape(snapshots * 2, SHELLS)
    total_cross, own_spectrum = packed_total((partial_cross, energy_own), "slab")
    all_spectra = gathered_copies(own_spectrum, TM, 0)
    order_hot = (ref_order[:, None] == jnp.arange(snapshots, dtype=jnp.int32)[None, :]).astype(
        jnp.float32
    )
    chosen = jnp.einsum(
        "js,spk->jpk",
        order_hot,
        total_cross.reshape(snapshots, 2, SHELLS),
        precision=lax.Precision.HIGHEST,
    )
    ref_energy = jnp.dot(
        order_hot, all_spectra, precision=lax.Precision.HIGHEST, preferred_element_type=jnp.float32
    )
    power_sum = chosen[:, 0] * chosen[:, 0] + chosen[:, 1] * chosen[:, 1]
    coherence = power_sum / (own_spectrum * ref_energy)
    return (coherence[None], own_spectrum)


def solution(mesh):
    split = Mesh(mesh.devices.reshape(8, 2, mesh.shape["slab"]), ("tm_0", "tm_1", "slab"))
    in_specs = (P(TM, None, None, "slab"), P("slab"), P())
    out_specs = (P(TM, None, None), P(TM, None))
    return jax.shard_map(body, mesh=split, in_specs=in_specs, out_specs=out_specs, check_vma=False)
```

profile of v0, /device:TPU:1, one launch (start us, length us, event | category | flops | bytes accessed | tf_op | source)
XLA Modules:
  0.0 114.2 jit_solution(11249714009123778423)
XLA Ops:
  0.6 1.1 copy.110
  1.7 16.2 %all_to_all.26 = bf16[8,2,1,3,2,1024]{5,4,3,1,2,0:T(2,128)(2,1)S(1)} all-to-all(bf16[8,2,1,3,2,1024]{5,4,3,1,2,0:T(2,128)(2,1)S(1)} %bitcast.51), channel_id=1, replica_groups=mesh['tm_0'=8,'tm_1'=2,'slab'=32] {'tm_0'}, dimensions={0} | all-to-all | bytes 393216 | tf_op jit(solution)/shard_map/all_to_all | solution.py:28
  17.9 0.8 copy.88
  18.7 3.6 %all-to-all-start.1 = ((bf16[8,2,1,3,2,1024]{5,4,3,0,2,1:T(2,128)(2,1)}), bf16[8,2,1,3,2,1024]{5,4,3,0,2,1:T(2,128)(2,1)S(1)}, u32[]{:S(2)}, u32[]{:S(2)}) async-start(bf16[8,2,1,3,2,1024]{5,4,3,0,2,1:T(2,128)(2,1)} %copy.88), calls=%async_computation.1 | async-start | bytes 393216 | tf_op jit(solution)/shard_map/all_to_all | solution.py:28
  22.3 0.7 dynamic_slice.3
  23.0 3.7 %all-to-all-done.1 = bf16[8,2,1,3,2,1024]{5,4,3,0,2,1:T(2,128)(2,1)S(1)} async-done(((bf16[8,2,1,3,2,1024]{5,4,3,0,2,1:T(2,128)(2,1)}), bf16[8,2,1,3,2,1024]{5,4,3,0,2,1:T(2,128)(2,1)S(1)}, u32[]{:S(2)}, u32[]{:S(2)}) %all-to-all-start.1) | async-done | bytes 196640 | tf_op jit(solution)/shard_map/all_to_all | solution.py:28
  26.7 0.1 copy.89
  26.8 1.4 %copy.90 = bf16[16,3,2,1024]{0,1,2,3:T(4,128)(2,1)S(1)} copy(bf16[16,3,2,1024]{3,2,1,0:T(2,128)(2,1)S(1)} %bitcast.50) | data formatting | bytes 393216 | tf_op jit(solution)/shard_map/reshape;reshape | solution.py:21
  28.2 1.7 %fusion.18 = (bf16[16,3,1,1024]{0,1,2,3:T(4,128)(2,1)S(1)}, bf16[16,3,1,1024]{0,1,2,3:T(4,128)(2,1)}) fusion(bf16[16,3,2,1024]{0,1,2,3:T(4,128)(2,1)S(1)} %copy.90), kind=kLoop, calls=%fused_computation.34 | loop fusion | flops 49152 | bytes 393216 | tf_op jit(solution)/shard_map/slice | solution.py:103
  29.9 4.4 %convolution_bitcast_fusion.1 = bf16[1024,16,16]{2,1,0:T(8,128)(2,1)} fusion(bf16[16,3,2,1024]{0,1,2,3:T(4,128)(2,1)S(1)} %copy.90), kind=kOutput, calls=%fused_computation.1 | convolution fusion | flops 3145728 | bytes 720896 | tf_op jit(solution)/shard_map/tcpm,rcpm->trm/dot_general | solution.py:104
  34.4 0.3 multiply_reduce_fusion
  34.8 6.0 %convolution_bitcast_fusion = bf16[1024,16,16]{2,1,0:T(8,128)(2,1)} fusion(bf16[16,3,2,1024]{0,1,2,3:T(4,128)(2,1)S(1)} %copy.90, bf16[16,3,1,1024]{0,1,2,3:T(4,128)(2,1)} %get-tuple-element.17, bf16[16,3,1,1024]{0,1,2,3:T(4,128)(2,1)S(1)} %get-tuple-element.16), kind=kOutput, calls=%fused_computation | convolution fusion | flops 3538944 | bytes 917504 | tf_op jit(solution)/shard_map/tcpm,rcpm->trm/dot_general | solution.py:107
  40.7 4.4 %copy.96 = bf16[1024,16,16]{0,2,1:T(8,128)(2,1)S(1)} copy(bf16[1024,16,16]{2,1,0:T(8,128)(2,1)} %convolution_bitcast_fusion) | data formatting | bytes 1048576 | tf_op jit(solution)/shard_map/tcpm,rcpm->trm/dot_general | solution.py:107
  45.1 4.9 %copy.92 = bf16[1024,16,16]{0,1,2:T(8,128)(2,1)S(1)} copy(bf16[1024,16,16]{2,1,0:T(8,128)(2,1)} %convolution_bitcast_fusion.1) | data formatting | bytes 1048576 | tf_op jit(solution)/shard_map/tcpm,rcpm->trm/dot_general | solution.py:104
  50.1 0.1 pad_maximum_fusion
  50.2 1.1 copy.97
  51.3 0.4 convert_element_type.18
  51.7 0.3 fusion.5
  52.0 0.6 fusion.6
  52.6 0.1 reshape.48
  52.7 0.0 copy-start
  52.7 0.2 reshape.49
  52.9 12.5 %all_to_all.27 = f32[16,1,4224]{2,1,0:T(1,128)S(1)} all-to-all(f32[16,1,4224]{2,1,0:T(1,128)S(1)} %reshape.49), channel_id=1, replica_groups=mesh['tm_0'=8,'tm_1'=2,'slab'=32] {'tm_0','tm_1'}, dimensions={0} | all-to-all | bytes 540672 | tf_op jit(solution)/shard_map/all_to_all | solution.py:39
  65.5 0.2 reduce_sum.30
  65.7 0.3 broadcast_in_dim.10
  66.0 35.2 %all_to_all.28 = f32[32,1,4224]{2,1,0:T(1,128)S(1)} all-to-all(f32[32,1,4224]{2,1,0:T(1,128)S(1)} %broadcast_in_dim.10), channel_id=1, replica_groups=mesh['tm_0'=8,'tm_1'=2,'slab'=32] {'slab'}, dimensions={0} | all-to-all | bytes 1081344 | tf_op jit(solution)/shard_map/all_to_all | solution.py:54
  101.2 0.3 reduce_sum.32
  101.5 0.5 slice_bitcast_fusion.1
  102.1 0.6 broadcast_in_dim.11
  102.7 3.5 %all-to-all-start.4 = ((f32[16,1,128]{2,1,0:T(1,128)}), f32[16,1,128]{2,1,0:T(1,128)S(1)}, u32[]{:S(2)}, u32[]{:S(2)}) async-start(f32[16,1,128]{2,1,0:T(1,128)} %broadcast_in_dim.11), calls=%async_computation.4 | async-start | bytes 16384 | tf_op jit(solution)/shard_map/all_to_all | solution.py:54
  106.1 0.0 copy-done
  106.1 0.2 fusion.9
  106.3 7.0 %all-to-all-done.4 = f32[16,1,128]{2,1,0:T(1,128)S(1)} async-done(((f32[16,1,128]{2,1,0:T(1,128)}), f32[16,1,128]{2,1,0:T(1,128)S(1)}, u32[]{:S(2)}, u32[]{:S(2)}) %all-to-all-start.4) | async-done | bytes 8224 | tf_op jit(solution)/shard_map/all_to_all | solution.py:54
  113.4 0.8 fusion.4
  (8 shorter events, 0.1 us)
Async XLA Ops:
  18.7 8.0 %all-to-all-start.1 = ((bf16[8,2,1,3,2,1024]{5,4,3,0,2,1:T(2,128)(2,1)}), bf16[8,2,1,3,2,1024]{5,4,3,0,2,1:T(2,128)(2,1)S(1)}, u32[]{:S(2)}, u32[]{:S(2)}) async-start(bf16[8,2,1,3,2,1024]{5,4,3,0,2,1:T(2,128)(2,1)} %copy.88), calls=%async_computation.1 | async-start | bytes 393216 | tf_op jit(solution)/shard_map/all_to_all | solution.py:28
  52.7 53.5 %copy-start = (s32[16]{0:T(128)S(1)}, s32[16]{0:T(128)}, u32[]{:S(2)}) copy-start(s32[16]{0:T(128)} %param.5) | copy-start | bytes 196
  102.7 10.7 %all-to-all-start.4 = ((f32[16,1,128]{2,1,0:T(1,128)}), f32[16,1,128]{2,1,0:T(1,128)S(1)}, u32[]{:S(2)}, u32[]{:S(2)}) async-start(f32[16,1,128]{2,1,0:T(1,128)} %broadcast_in_dim.11), calls=%async_computation.4 | async-start | bytes 16384 | tf_op jit(solution)/shard_map/all_to_all | solution.py:54
where the time goes:
time: 115 us; the launch traced here: 114 us
  blocking collectives  64 us (56%)
  local copies, waits for them, and re-layouts  16.7 us (15%)
  matrix products  12.3 us (11%)
  waiting for transfers between devices  10.7 us (9%)
  starting transfers between devices  7.1 us (6%)
  other arithmetic  2.63 us (2%)
    all_to_all x1, blocking collectives, copy_for_each(): lax.all_to_all(jnp.broadcast_to(array[None], (devices, *array.shape)), ax...  35.2 us
    all_to_all x1, blocking collectives, turned_blocks(): whole = lax.all_to_all(whole, axes[k], k, k, tiled=True)  16.2 us
    all_to_all x1, blocking collectives, sum_at_owner(): lax.all_to_all(cut_along(array, dim, devices), axis, 0, 0, tiled=True)  12.5 us
    all_to_all x1, waiting for transfers between devices, copy_for_each(): lax.all_to_all(jnp.broadcast_to(array[None], (devices, *array.shape)), ax...  7.04 us
    dot_general x1, matrix products, body(): jnp.einsum('tcpm,rcpm->trm', rotated, local_modes, preferred_element_type...  5.98 us
    dot_general x1, local copies, waits for them, and re-layouts, body(): jnp.einsum('tcpm,rcpm->trm', local_modes, local_modes, preferred_element_...  4.94 us
    dot_general x1, matrix products, body(): jnp.einsum('tcpm,rcpm->trm', local_modes, local_modes, preferred_element_...  4.41 us
    dot_general x1, local copies, waits for them, and re-layouts, body(): jnp.einsum('tcpm,rcpm->trm', rotated, local_modes, preferred_element_type...  4.4 us
  transfers between devices with their start and end apart: 2, of which 2 were waited for; matrix products, arithmetic and copies ran while one was open for 1% of the time, Pallas kernels for 0%

commit v1 on v0

v1 whole, which is shorter than its diff:
```python
import functools

import jax
import jax.numpy as jnp
from jax import lax
from jax.experimental import pallas as pl
from jax.experimental.pallas import tpu as pltpu
from jax.sharding import PartitionSpec as P

SHELLS = 128
LANES = 128
Z_LO, Z_HI, CORES = 2, 4, 2
MESH = pl.DeviceIdType.MESH
ROWS = 16
GROUPS = ROWS // 2
PITCH = ROWS + 1


def remote(src, dst, send_sem, recv_sem, tm, slab):
    return pltpu.make_async_remote_copy(
        src_ref=src,
        dst_ref=dst,
        send_sem=send_sem,
        recv_sem=recv_sem,
        device_id={"tm": tm, "slab": slab},
        device_id_type=MESH,
    )


def kernel(
    sizes,
    vel_ref,
    shell_ref,
    order_ref,
    coh_ref,
    spec_ref,
    src,
    recv,
    ids,
    wide,
    terms,
    onehot,
    sums,
    peer_sums,
    y_recv,
    x_recv,
    z_src,
    z_recv,
    own_msg,
    c_recv,
    coh_rows,
    load_sem,
    m_send,
    m_recv,
    d_send,
    d_recv,
    y_send,
    y_rsem,
    x_send,
    x_rsem,
    z_send,
    z_rsem,
    c_send,
    c_rsem,
    o_send,
    o_rsem,
):
    y_n, x_n, z_hi_n, z_lo_n = sizes
    snaps = y_n * z_lo_n
    half = snaps // 2
    z_n = z_hi_n * z_lo_n
    block = z_lo_n * snaps
    me = lax.axis_index("tm")
    slab = lax.axis_index("slab")
    y, z_lo = me // z_lo_n, me % z_lo_n
    core = slab % CORES
    chip_slab = slab // CORES
    x, z_hi = chip_slab // z_hi_n, chip_slab % z_hi_n
    z = z_hi * z_lo_n + z_lo
    far = slab - core
    near = far + 1

    def slab_of(xx, zz, cc):
        return (xx * z_hi_n + zz) * CORES + cc

    load_all = pltpu.make_async_copy(vel_ref, src, load_sem.at[0])
    load_all.start()
    mine = pl.ds(pl.multiple_of(me * ROWS, ROWS), ROWS)
    load_own = pltpu.make_async_copy(vel_ref.at[:, mine], recv.at[me], load_sem.at[1])
    load_own.start()
    load_ids = pltpu.make_async_copy(
        shell_ref.at[pl.ds(pl.multiple_of(me * GROUPS, GROUPS), GROUPS)], ids, load_sem.at[2]
    )
    load_ids.start()

    barrier = pltpu.get_barrier_semaphore()

    def greet(tm, sl):
        pl.semaphore_signal(barrier, inc=1, device_id={"tm": tm, "slab": sl}, device_id_type=MESH)

    for d in range(1, snaps):
        greet((me + d) % snaps, slab)

    @pl.when(core == 0)
    def _():
        greet(me, near)
        for d in range(1, snaps):
            greet((me + d) % snaps, near)
        pl.semaphore_wait(barrier, snaps)

    z_partners = [(zl, dz) for zl in range(z_lo_n) for dz in range(z_hi_n) if (zl, dz) != (0, 0)]

    @pl.when(core == 1)
    def _():
        greet(me, far)
        for d in range(1, x_n):
            greet(me, slab_of((x + d) % x_n, z_hi, 1))
        for zl, dz in z_partners:
            if dz:
                greet(y * z_lo_n + (z_lo + zl) % z_lo_n, slab_of(x, (z_hi + dz) % z_hi_n, 1))
        others = sum(1 for _, dz in z_partners if dz)
        pl.semaphore_wait(barrier, 2 * snaps - 1 + x_n - 1 + others)

    load_all.wait()
    m_copies = []
    for d in range(1, snaps):
        to = (me + d) % snaps
        part = pl.ds(pl.multiple_of(to * ROWS, ROWS), ROWS)
        copy = remote(src.at[:, part], recv.at[me], m_send.at[d], m_recv.at[d], to, slab)
        copy.start()
        m_copies.append(copy)

    load_ids.wait()
    shells = lax.broadcasted_iota(jnp.int32, (SHELLS, LANES), 0)
    for g in range(GROUPS):
        row = jnp.broadcast_to(ids[g : g + 1, :], (SHELLS, LANES))
        onehot[:, g * LANES : (g + 1) * LANES] = jnp.where(row == shells, 1.0, 0.0).astype(
            jnp.bfloat16
        )

    load_own.wait()
    for d in range(1, snaps):
        frm = (me + snaps - d) % snaps
        remote(
            src.at[:, pl.ds(0, ROWS)], recv.at[frm], m_send.at[d], m_recv.at[d], me, slab
        ).wait_recv()
    for t in range(snaps):
        for c in range(3):
            value = recv[t, c].astype(jnp.float32)
            wide[c, t * PITCH : t * PITCH + ROWS, :] = value
            if t < half:
                at = (t + snaps) * PITCH
                wide[c, at : at + ROWS, :] = value

    first = lax.broadcasted_iota(jnp.int32, (snaps, LANES), 0) < half
    for g in range(GROUPS):

        def rows(c, p, d):
            return wide[c, pl.ds(d * PITCH + 2 * g + p, snaps, stride=PITCH), :]

        own = [[rows(c, p, 0) for p in range(2)] for c in range(3)]

        def put(k, value):
            terms[k * snaps : (k + 1) * snaps, g * LANES : (g + 1) * LANES] = value.astype(
                jnp.bfloat16
            )

        put(0, sum(own[c][p] * own[c][p] for c in range(3) for p in range(2)))
        for d in range(1, half + 1):
            other = [[rows(c, p, d) for p in range(2)] for c in range(3)]
            real = sum(own[c][p] * other[c][p] for c in range(3) for p in range(2))
            imag = sum(own[c][1] * other[c][0] - own[c][0] * other[c][1] for c in range(3))
            if d < half:
                put(2 * d - 1, real)
                put(2 * d, imag)
            else:
                put(2 * d - 1, jnp.where(first, real, imag))

    binned = lax.dot_general(
        terms[...], onehot[...], (((1,), (1,)), ((), ())), preferred_element_type=jnp.float32
    )
    for k in range(snaps):
        sums[pl.ds(k, snaps, stride=snaps), :] = binned[k * snaps : (k + 1) * snaps]

    def to_near():
        return remote(sums, peer_sums, d_send, d_recv, me, near)

    @pl.when(core == 0)
    def _():
        to_near().start()

    @pl.when(core == 1)
    def _():
        to_near().wait_recv()
        sums[...] += peer_sums[...]

        def y_block(yy):
            return pl.ds(pl.multiple_of(yy * block, block), block)

        for d in range(1, y_n):
            yy = (y + d) % y_n
            remote(
                sums.at[y_block(yy)],
                y_recv.at[y],
                y_send.at[d],
                y_rsem.at[d],
                yy * z_lo_n + z_lo,
                slab,
            ).start()
        y_recv[y] = sums[y_block(y), :]
        for d in range(1, y_n):
            frm = (y + y_n - d) % y_n
            remote(
                sums.at[y_block(0)], y_recv.at[frm], y_send.at[d], y_rsem.at[d], me, slab
            ).wait_recv()
        x_recv[x] = sum((y_recv[i] for i in range(1, y_n)), y_recv[0])

        for d in range(1, x_n):
            xx = (x + d) % x_n
            remote(
                x_recv.at[x], x_recv.at[x], x_send.at[d], x_rsem.at[d], me, slab_of(xx, z_hi, 1)
            ).start()
        for d in range(1, x_n):
            frm = (x + x_n - d) % x_n
            remote(
                x_recv.at[x], x_recv.at[frm], x_send.at[d], x_rsem.at[d], me, slab
            ).wait_recv()
        over_x = sum((x_recv[i] for i in range(1, x_n)), x_recv[0])
        for i in range(z_lo_n):
            z_src[i] = over_x[i * snaps : (i + 1) * snaps]

        for n, (zl, dz) in enumerate(z_partners):
            to_lo, to_hi = (z_lo + zl) % z_lo_n, (z_hi + dz) % z_hi_n
            remote(
                z_src.at[to_lo],
                z_recv.at[z],
                z_send.at[n],
                z_rsem.at[n],
                y * z_lo_n + to_lo,
                slab_of(x, to_hi, 1),
            ).start()
        z_recv[z] = z_src[z_lo]
        for n, (zl, dz) in enumerate(z_partners):
            from_lo, from_hi = (z_lo + z_lo_n - zl) % z_lo_n, (z_hi + z_hi_n - dz) % z_hi_n
            frm = from_hi * z_lo_n + from_lo
            remote(
                z_src.at[0], z_recv.at[frm], z_send.at[n], z_rsem.at[n], me, slab
            ).wait_recv()
        total = sum((z_recv[i] for i in range(1, z_n)), z_recv[0])

        own_spec = total[0:1]
        for d in range(snaps):
            own_msg[d, 0:1, :] = own_spec
            if 0 < d < half:
                re, im = total[2 * d - 1 : 2 * d], total[2 * d : 2 * d + 1]
                own_msg[d, 1:2, :] = re * re + im * im
            elif d == half:
                row = total[2 * d - 1 : 2 * d]
                own_msg[d, 1:2, :] = row * row
            else:
                own_msg[d, 1:2, :] = own_spec * own_spec
        for d in range(1, snaps):
            to = (me + d) % snaps
            for cc in range(CORES):
                remote(
                    own_msg.at[d], c_recv.at[d], c_send.at[cc, d], c_rsem.at[d], to, far + cc
                ).start()
        remote(own_msg, own_msg, o_send, o_rsem, me, far).start()

    @pl.when(core == 0)
    def _():
        remote(own_msg, own_msg, o_send, o_rsem, me, near).wait_recv()

    for d in range(1, snaps):
        remote(own_msg.at[d], c_recv.at[d], c_send.at[0, d], c_rsem.at[d], me, slab).wait_recv()

    spec = own_msg[0, 0:1, :]
    spec_ref[...] = spec
    coh_rows[0] = own_msg[0, 1:2, :] / (spec * spec)
    for e in range(1, snaps):
        if e < half:
            power = c_recv[e, 1:2, :]
        elif e == half:
            power = c_recv[e, 1:2, :] + own_msg[e, 1:2, :]
        else:
            power = own_msg[snaps - e, 1:2, :]
        coh_rows[e] = power / (spec * c_recv[e, 0:1, :])
    for j in range(snaps):
        coh_ref[0, j : j + 1, :] = coh_rows[(me - order_ref[j] + snaps) % snaps]

    for copy in m_copies:
        copy.wait_send()

    @pl.when(core == 0)
    def _():
        to_near().wait_send()

    @pl.when(core == 1)
    def _():
        for d in range(1, y_n):
            remote(
                sums.at[pl.ds(0, block)], y_recv.at[0], y_send.at[d], y_rsem.at[d], me, slab
            ).wait_send()
        for d in range(1, x_n):
            remote(x_recv.at[x], x_recv.at[x], x_send.at[d], x_rsem.at[d], me, slab).wait_send()
        for n in range(len(z_partners)):
            remote(z_src.at[0], z_recv.at[0], z_send.at[n], z_rsem.at[n], me, slab).wait_send()
        for d in range(1, snaps):
            for cc in range(CORES):
                remote(
                    own_msg.at[d], c_recv.at[d], c_send.at[cc, d], c_rsem.at[d], me, slab
                ).wait_send()
        remote(own_msg, own_msg, o_send, o_rsem, me, far).wait_send()


def body(sizes, velocity, shell_index, ref_order):
    y_n, x_n, z_hi_n, z_lo_n = sizes
    snaps = y_n * z_lo_n
    half = snaps // 2
    z_n = z_hi_n * z_lo_n
    lanes_n = velocity.shape[3] // LANES
    vel = velocity.reshape(3, 2, lanes_n, LANES).transpose(0, 2, 1, 3)
    vel = vel.reshape(3, 2 * lanes_n, LANES)
    ids = shell_index.reshape(lanes_n, LANES)
    f32, dma = jnp.float32, pltpu.SemaphoreType.DMA
    return pl.pallas_call(
        functools.partial(kernel, sizes),
        out_shape=(
            jax.ShapeDtypeStruct((1, snaps, SHELLS), f32),
            jax.ShapeDtypeStruct((1, SHELLS), f32),
        ),
        in_specs=[
            pl.BlockSpec(memory_space=pl.ANY),
            pl.BlockSpec(memory_space=pl.ANY),
            pl.BlockSpec(memory_space=pltpu.SMEM),
        ],
        out_specs=(pl.BlockSpec(memory_space=pltpu.VMEM), pl.BlockSpec(memory_space=pltpu.VMEM)),
        scratch_shapes=[
            pltpu.VMEM((3, 2 * lanes_n, LANES), jnp.bfloat16),
            pltpu.VMEM((snaps, 3, ROWS, LANES), jnp.bfloat16),
            pltpu.VMEM((GROUPS, LANES), jnp.int32),
            pltpu.VMEM((3, (snaps + half + 1) * PITCH, LANES), f32),
            pltpu.VMEM((snaps * snaps, GROUPS * LANES), jnp.bfloat16),
            pltpu.VMEM((SHELLS, GROUPS * LANES), jnp.bfloat16),
            pltpu.VMEM((snaps * snaps, SHELLS), f32),
            pltpu.VMEM((snaps * snaps, SHELLS), f32),
            pltpu.VMEM((y_n, z_lo_n * snaps, SHELLS), f32),
            pltpu.VMEM((x_n, z_lo_n * snaps, SHELLS), f32),
            pltpu.VMEM((z_lo_n, snaps, SHELLS), f32),
            pltpu.VMEM((z_n, snaps, SHELLS), f32),
            pltpu.VMEM((snaps, 2, SHELLS), f32),
            pltpu.VMEM((snaps, 2, SHELLS), f32),
            pltpu.VMEM((snaps, 1, SHELLS), f32),
            dma((3,)),
            dma((snaps,)),
            dma((snaps,)),
            dma(()),
            dma(()),
            dma((y_n,)),
            dma((y_n,)),
            dma((x_n,)),
            dma((x_n,)),
            dma((z_n,)),
            dma((z_n,)),
            dma((CORES, snaps)),
            dma((snaps,)),
            dma(()),
            dma(()),
        ],
        compiler_params=pltpu.CompilerParams(collective_id=0, has_side_effects=True),
    )(vel, ids, ref_order)


def solution(mesh):
    tm, slab = mesh.shape["tm"], mesh.shape["slab"]
    z_hi_n = min(Z_HI, slab // CORES)
    sizes = (tm // Z_LO, slab // CORES // z_hi_n, z_hi_n, Z_LO)
    return jax.shard_map(
        functools.partial(body, sizes),
        mesh=mesh,
        in_specs=(P("tm", None, None, "slab"), P("slab"), P()),
        out_specs=(P("tm", None, None), P("tm", None)),
        check_vma=False,
    )
```

time: 115 us -> 45.9 us (0.40)
  blocking collectives: 64 us -> 0 us
  Pallas kernels: 0 us -> 43.3 us
  local copies, waits for them, and re-layouts: 16.7 us -> 1.81 us
  matrix products: 12.3 us -> 0 us
  waiting for transfers between devices: 10.7 us -> 0 us
  starting transfers between devices: 7.1 us -> 0 us
  other arithmetic: 2.63 us -> 0 us
    all_to_all x3 -> x0, blocking collectives: 64 us -> none  [the longest x1 35.2 us: copy_for_each(): lax.all_to_all(jnp.broadcast_to(array[None], (devices, *array.shape)), ax...]
    pallas_call x0 -> x1, Pallas kernels: none -> 43.3 us  [body(): pl.pallas_call(functools.partial(kernel, sizes), out_shape=(jax.ShapeDtyp...]
    dot_general x6 -> x0, matrix products: 12.3 us -> none  [the longest x1 5.98 us: body(): jnp.einsum('tcpm,rcpm->trm', rotated, local_modes, preferred_element_type...]
    all_to_all x2 -> x0, waiting for transfers between devices: 10.7 us -> none  [the longest x1 7.04 us: copy_for_each(): lax.all_to_all(jnp.broadcast_to(array[None], (devices, *array.shape)), ax...]
    dot_general x2 -> x0, local copies, waits for them, and re-layouts: 9.34 us -> none  [the longest x1 4.94 us: body(): jnp.einsum('tcpm,rcpm->trm', local_modes, local_modes, preferred_element_...]
    all_to_all x2 -> x0, starting transfers between devices: 7.1 us -> none  [the longest x1 3.63 us: turned_blocks(): whole = lax.all_to_all(whole, axes[k], k, k, tiled=True)]
    another operation x2 -> x0, local copies, waits for them, and re-layouts: 2.52 us -> none  [the longest x1 1.44 us: in_order(): parts.reshape(*shape[:dim], shape[dim] * shape[dim + 1], *shape[dim + 2:])]
    reshape x5 -> x0, local copies, waits for them, and re-layouts: 1.82 us -> none  [the longest x2 1.25 us: cut_along(): return jnp.moveaxis(array.reshape(*before, devices, -1, *after), dim, 0)]
  transfers between devices with their start and end apart: 2 -> 0, of which waited for: 2 -> 0; matrix products, arithmetic and copies ran while one was open for 1% -> 0% of each run, Pallas kernels for 0% -> 0%
where the time goes in v1:
time: 45.9 us; the launch traced here: 45.7 us
  Pallas kernels  43.3 us (94%)
  local copies, waits for them, and re-layouts  1.81 us (4%)
  between operations  0.65 us (1%)
    pallas_call x1, Pallas kernels, body(): pl.pallas_call(functools.partial(kernel, sizes), out_shape=(jax.ShapeDtyp...  43.3 us
    unnamed x4, local copies, waits for them, and re-layouts  1.81 us

profile of v1, /device:TPU:1, one launch (start us, length us, event | category | flops | bytes accessed | tf_op | source)
XLA Modules:
  0.0 45.7 jit_solution(3697442321741248851)
XLA Ops:
  0.6 43.3 %shard_map.50 = (f32[1,16,128]{2,1,0:T(8,128)}, f32[1,128]{1,0:T(1,128)}) custom-call(bf16[3,256,128]{2,1,0:T(8,128)(2,1)} %bitcast.6, s32[128,128]{1,0:T(8,128)} %bitcast.7, s32[16]{0:T(128)} %order_ref.1), custom_call_target="tpu_custom_call" | custom-call | tf_op jit(solution)/shard_map/pallas_call | solution.py:326
  43.9 0.0 copy-start
  43.9 1.3 %copy.8 = f32[1,16,128]{2,1,0:T(8,128)} copy(f32[1,16,128]{2,1,0:T(8,128)} %get-tuple-element.4) | data formatting | bytes 16384
  45.2 0.0 copy-done
  45.2 0.5 %copy.9 = f32[1,128]{1,0:T(1,128)} copy(f32[1,128]{1,0:T(1,128)S(1)} %copy-done) | data formatting | bytes 1024
Async XLA Ops:
  43.9 1.3 %copy-start = (f32[1,128]{1,0:T(1,128)S(1)}, f32[1,128]{1,0:T(1,128)}, u32[]{:S(2)}) copy-start(f32[1,128]{1,0:T(1,128)} %get-tuple-element.5) | copy-start | bytes 1540

commit v2 on v0

v2 whole, which is shorter than its diff:
```python
import functools

import jax
import jax.numpy as jnp
from jax import lax
from jax.experimental import pallas as pl
from jax.experimental.pallas import tpu as pltpu
from jax.sharding import PartitionSpec as P

SHELLS = 128
LANES = 128
Z_LO, Z_HI, CORES = 2, 4, 2
ROWS = 16
GROUPS = ROWS // 2
PITCH = ROWS + 1
OUT_ROWS = 24


def remote(src, dst, send_sem, recv_sem, tm, slab):
    return pltpu.make_async_remote_copy(
        src_ref=src,
        dst_ref=dst,
        send_sem=send_sem,
        recv_sem=recv_sem,
        device_id={"tm": tm, "slab": slab},
        device_id_type=pl.DeviceIdType.MESH,
    )


def ordered_sum(terms):
    total = terms[0]
    for term in terms[1:]:
        total = total + term
    return total


def kernel(
    sizes,
    vel_ref,
    shell_ref,
    order_hbm,
    out_ref,
    src,
    recv,
    ids,
    order_ref,
    wide,
    terms,
    onehot,
    sums,
    r_recv,
    x_recv,
    own_src,
    own_recv,
    pair_src,
    pair_recv,
    coh_rows,
    final,
    load_sem,
    m_send,
    m_recv,
    i_send,
    i_recv,
    r_send,
    r_rsem,
    x_send,
    x_rsem,
    p_send,
    p_rsem,
    f_send,
    f_rsem,
):
    snaps, x_n, z_hi_n = sizes
    half = snaps // 2
    heads = min(2, z_hi_n)
    me = lax.axis_index("tm")
    slab = lax.axis_index("slab")
    core = slab % CORES
    x, z_hi = slab // CORES // z_hi_n, slab // CORES % z_hi_n
    far = slab - core
    near = far + 1
    by_distance = sorted(range(1, snaps), key=lambda d: (-min(d, snaps - d), d))

    def there(d):
        return (me + d) % snaps

    def whence(d):
        return (me + snaps - d) % snaps

    def slab_of(xx, zz, cc):
        return (xx * z_hi_n + zz) * CORES + cc

    def rows_of(t, n):
        return pl.ds(pl.multiple_of(t * n, n), n)

    load_all = pltpu.make_async_copy(vel_ref, src, load_sem.at[0])
    load_all.start()
    load_ids = pltpu.make_async_copy(
        shell_ref.at[rows_of(me, GROUPS)], ids.at[core], load_sem.at[1]
    )
    load_own = pltpu.make_async_copy(
        vel_ref.at[:, rows_of(me, ROWS)], recv.at[1, me], load_sem.at[2]
    )
    load_order = pltpu.make_async_copy(order_hbm, order_ref, load_sem.at[3])

    barrier = pltpu.get_barrier_semaphore()

    def greet(tm, sl):
        pl.semaphore_signal(
            barrier, inc=1, device_id={"tm": tm, "slab": sl}, device_id_type=pl.DeviceIdType.MESH
        )

    with jax.named_scope("a_greet"):

        @pl.when(core == 1)
        def _():
            for d in by_distance:
                greet(there(d), near)
                greet(there(d), far)
            greet(me, far)
            for d in range(1, x_n):
                greet(there(0), slab_of((x + d) % x_n, z_hi, 1))

        load_ids.start()

        @pl.when(core == 1)
        def _():
            load_own.start()
            load_order.start()

            @pl.when(z_hi < heads)
            def _():
                for h in range(1, z_hi_n):
                    for d in range(snaps):
                        greet(there(d), slab_of(x, (z_hi + h) % z_hi_n, 1))

    with jax.named_scope("b_barrier"):

        @pl.when(core == 0)
        def _():
            pl.semaphore_wait(barrier, snaps)

        @pl.when(core == 1)
        def _():
            @pl.when(z_hi < heads)
            def _():
                pl.semaphore_wait(barrier, snaps - 1 + x_n - 1 + (heads - 1) * snaps)

            @pl.when(z_hi >= heads)
            def _():
                pl.semaphore_wait(barrier, snaps - 1 + x_n - 1 + heads * snaps)

    def part_copy(d):
        return remote(
            src.at[:, rows_of(there(d), ROWS)],
            recv.at[core, me],
            m_send.at[d],
            m_recv.at[core, d],
            there(d),
            near,
        )

    def ids_copy():
        return remote(ids.at[0], ids.at[0], i_send, i_recv, me, near)

    load_all.wait()
    for d in by_distance:
        part_copy(d).start()

    @pl.when(core == 0)
    def _():
        part_copy(0).start()
        load_ids.wait()
        ids_copy().start()

    @pl.when(core == 1)
    def _():
        shells = lax.broadcasted_iota(jnp.int32, (SHELLS, LANES), 0)
        first = lax.broadcasted_iota(jnp.int32, (snaps, LANES), 0) < half

        def spread_shells(c):
            for g in range(GROUPS):
                row = jnp.broadcast_to(ids[c, g : g + 1, :], (SHELLS, LANES))
                hot = jnp.where(row == shells, 1.0, 0.0).astype(jnp.bfloat16)
                onehot[c, :, g * LANES : (g + 1) * LANES] = hot

        def widen(core_of):
            for t in range(snaps):
                for c in range(3):
                    value = recv[core_of, t, c].astype(jnp.float32)
                    wide[c, t * PITCH : t * PITCH + ROWS, :] = value
                    if t < half:
                        at = (t + snaps) * PITCH
                        wide[c, at : at + ROWS, :] = value

        def products():
            for g in range(GROUPS):

                def rows(c, p, d):
                    return wide[c, pl.ds(d * PITCH + 2 * g + p, snaps, stride=PITCH), :]

                def put(k, value):
                    terms[k * snaps : (k + 1) * snaps, g * LANES : (g + 1) * LANES] = value.astype(
                        jnp.bfloat16
                    )

                own = [[rows(c, p, 0) for p in range(2)] for c in range(3)]
                put(0, sum(own[c][p] * own[c][p] for c in range(3) for p in range(2)))
                for d in range(1, half + 1):
                    other = [[rows(c, p, d) for p in range(2)] for c in range(3)]
                    real = sum(own[c][p] * other[c][p] for c in range(3) for p in range(2))
                    imag = sum(own[c][1] * other[c][0] - own[c][0] * other[c][1] for c in range(3))
                    if d < half:
                        put(2 * d - 1, real)
                        put(2 * d, imag)
                    else:
                        put(2 * d - 1, jnp.where(first, real, imag))

        def binned(c):
            return lax.dot_general(
                terms[...],
                onehot[c],
                (((1,), (1,)), ((), ())),
                preferred_element_type=jnp.float32,
            )

        def wait_part(c, d):
            remote(
                src.at[:, pl.ds(0, ROWS)],
                recv.at[c, whence(d)],
                m_send.at[d],
                m_recv.at[c, d],
                me,
                slab,
            ).wait_recv()

        with jax.named_scope("c_onehot"):
            load_ids.wait()
            spread_shells(1)
            ids_copy().wait_recv()
            spread_shells(0)
        with jax.named_scope("d_wait1"):
            load_own.wait()
            for d in reversed(by_distance):
                wait_part(1, d)
        with jax.named_scope("e_work1"):
            widen(1)
            products()
            sums[...] = binned(1)
        with jax.named_scope("f_wait0"):
            for d in [0, *reversed(by_distance)]:
                wait_part(0, d)
        with jax.named_scope("g_work0"):
            widen(0)
            products()
            both = sums[...] + binned(0)
            for k in range(snaps):
                sums[pl.ds(k, snaps, stride=snaps), :] = both[k * snaps : (k + 1) * snaps]

        with jax.named_scope("h_owner"):
            for d in by_distance:
                remote(
                    sums.at[rows_of(there(d), snaps)],
                    r_recv.at[me],
                    r_send.at[d],
                    r_rsem.at[d],
                    there(d),
                    slab,
                ).start()
            r_recv[me] = sums[rows_of(me, snaps), :]
            for d in reversed(by_distance):
                remote(
                    sums.at[pl.ds(0, snaps)],
                    r_recv.at[whence(d)],
                    r_send.at[d],
                    r_rsem.at[d],
                    me,
                    slab,
                ).wait_recv()
            x_recv[x] = ordered_sum([r_recv[t] for t in range(snaps)])

        with jax.named_scope("i_x"):
            for d in range(1, x_n):
                remote(
                    x_recv.at[x],
                    x_recv.at[x],
                    x_send.at[d],
                    x_rsem.at[d],
                    me,
                    slab_of((x + d) % x_n, z_hi, 1),
                ).start()
            for d in range(1, x_n):
                remote(
                    x_recv.at[x],
                    x_recv.at[(x + x_n - d) % x_n],
                    x_send.at[d],
                    x_rsem.at[d],
                    me,
                    slab,
                ).wait_recv()
            total = ordered_sum([x_recv[i] for i in range(x_n)])

        with jax.named_scope("j_pairs"):
            own_src[...] = total
            for d in range(1, snaps):
                pair_src[d, 0, 0:1, :] = total[0:1]
                if d < half:
                    pair_src[d, 1, :, :] = total[2 * d - 1 : 2 * d + 1]
                elif d == half:
                    pair_src[d, 1, 0:1, :] = total[2 * d - 1 : 2 * d]
                    pair_src[d, 1, 1:2, :] = jnp.zeros((1, SHELLS), jnp.float32)
                pair_src[d, 0, 1:2, :] = jnp.zeros((1, SHELLS), jnp.float32)

        def pair_ref(ref, d):
            return ref.at[d] if d <= half else ref.at[d, 0]

        def pair_send(h, d):
            return remote(
                pair_ref(pair_src, d),
                pair_ref(pair_recv.at[z_hi], d),
                p_send.at[h, d],
                p_rsem.at[z_hi, d],
                there(d),
                slab_of(x, h, 1),
            )

        def own_send(h):
            return remote(
                own_src,
                own_recv.at[z_hi],
                p_send.at[h, 0],
                p_rsem.at[z_hi, 0],
                me,
                slab_of(x, h, 1),
            )

        with jax.named_scope("k_send"):
            for h in range(heads):
                for d in by_distance:
                    pair_send(h, d).start()

                @pl.when(z_hi != h)
                def _(h=h):
                    own_send(h).start()

                @pl.when(z_hi == h)
                def _(h=h):
                    own_recv[h] = own_src[...]

        def to_late(c):
            return remote(
                final,
                final,
                f_send.at[c],
                f_rsem,
                me,
                slab_of(x, z_hi_n - 1 - z_hi, c),
            )

        def to_partner():
            return remote(final, final, f_send.at[2], f_rsem, me, far)

        @pl.when(z_hi < heads)
        def _():
            with jax.named_scope("l_pairwait"):
                for h in range(z_hi_n):
                    for d in reversed(by_distance):
                        remote(
                            pair_ref(pair_src, d),
                            pair_ref(pair_recv.at[h], d),
                            p_send.at[0, d],
                            p_rsem.at[h, d],
                            me,
                            slab,
                        ).wait_recv()

                    @pl.when(z_hi != h)
                    def _(h=h):
                        remote(
                            own_src, own_recv.at[h], p_send.at[0, 0], p_rsem.at[h, 0], me, slab
                        ).wait_recv()

            with jax.named_scope("m_coh"):
                load_order.wait()
                own = ordered_sum([own_recv[h] for h in range(z_hi_n)])
                spec = own[0:1]
                energy = [spec] + [
                    ordered_sum([pair_recv[h, d, 0, 0:1, :] for h in range(z_hi_n)])
                    for d in range(1, snaps)
                ]
                final[snaps : snaps + 1, :] = spec
                coh_rows[0] = spec * spec / (spec * spec)
                for e in range(1, snaps):
                    if e <= half:
                        pair = ordered_sum([pair_recv[h, e, 1] for h in range(z_hi_n)])
                        re, im = pair[0:1], pair[1:2]
                        if e == half:
                            im = own[2 * e - 1 : 2 * e]
                    else:
                        d = snaps - e
                        re, im = own[2 * d - 1 : 2 * d], own[2 * d : 2 * d + 1]
                    coh_rows[e] = (re * re + im * im) / (spec * energy[e])
                for j in range(snaps):
                    final[j : j + 1, :] = coh_rows[(me - order_ref[j] + snaps) % snaps]
                to_partner().start()

                @pl.when(z_hi_n - 1 - z_hi >= heads)
                def _():
                    for c in (1, 0):
                        to_late(c).start()

        @pl.when(z_hi >= heads)
        def _():
            with jax.named_scope("n_finalwait"):
                remote(final, final, f_send.at[0], f_rsem, me, slab).wait_recv()
                load_order.wait()

    @pl.when(core == 0)
    def _():
        with jax.named_scope("n_finalwait"):
            remote(final, final, f_send.at[0], f_rsem, me, slab).wait_recv()

    with jax.named_scope("o_end"):
        out_ref[...] = final[0 : snaps + 1]
        for d in by_distance:
            part_copy(d).wait_send()

        @pl.when(core == 0)
        def _():
            part_copy(0).wait_send()
            ids_copy().wait_send()

        @pl.when(core == 1)
        def _():
            for d in range(1, snaps):
                remote(
                    sums.at[pl.ds(0, snaps)], r_recv.at[0], r_send.at[d], r_rsem.at[d], me, slab
                ).wait_send()
            for d in range(1, x_n):
                remote(
                    x_recv.at[x], x_recv.at[x], x_send.at[d], x_rsem.at[d], me, slab
                ).wait_send()
            for h in range(heads):
                for d in range(1, snaps):
                    ref = pair_src.at[d] if d <= half else pair_src.at[d, 0]
                    remote(ref, ref, p_send.at[h, d], p_rsem.at[0, d], me, slab).wait_send()

                @pl.when(z_hi != h)
                def _(h=h):
                    remote(
                        own_src, own_src, p_send.at[h, 0], p_rsem.at[0, 0], me, slab
                    ).wait_send()

            @pl.when(z_hi < heads)
            def _():
                remote(final, final, f_send.at[2], f_rsem, me, slab).wait_send()

                @pl.when(z_hi_n - 1 - z_hi >= heads)
                def _():
                    for c in (1, 0):
                        remote(final, final, f_send.at[c], f_rsem, me, slab).wait_send()


def finish(snaps, done_ref, coh_ref, spec_ref, sem):
    coh = pltpu.make_async_copy(done_ref.at[0:snaps], coh_ref.at[0], sem.at[0])
    spec = pltpu.make_async_copy(done_ref.at[snaps : snaps + 1], spec_ref, sem.at[1])
    coh.start()
    spec.start()
    coh.wait()
    spec.wait()


def body(sizes, velocity, shell_index, ref_order):
    snaps, x_n, z_hi_n = sizes
    half = snaps // 2
    heads = min(2, z_hi_n)
    lanes_n = velocity.shape[3] // LANES
    vel = velocity.reshape(3, 2, lanes_n, LANES).transpose(0, 2, 1, 3)
    vel = vel.reshape(3, 2 * lanes_n, LANES)
    ids = shell_index.reshape(lanes_n, LANES)
    f32, bf16, dma = jnp.float32, jnp.bfloat16, pltpu.SemaphoreType.DMA
    done = pl.pallas_call(
        functools.partial(kernel, sizes),
        out_shape=pltpu.VMEM((snaps + 1, SHELLS), f32),
        in_specs=[pl.BlockSpec(memory_space=pl.ANY)] * 3,
        out_specs=pl.BlockSpec(memory_space=pltpu.VMEM),
        scratch_shapes=[
            pltpu.VMEM((3, 2 * lanes_n, LANES), bf16),
            pltpu.VMEM((CORES, snaps, 3, ROWS, LANES), bf16),
            pltpu.VMEM((CORES, GROUPS, LANES), jnp.int32),
            pltpu.SMEM((snaps,), jnp.int32),
            pltpu.VMEM((3, (snaps + half + 1) * PITCH, LANES), f32),
            pltpu.VMEM((snaps * snaps, GROUPS * LANES), bf16),
            pltpu.VMEM((CORES, SHELLS, GROUPS * LANES), bf16),
            pltpu.VMEM((snaps * snaps, SHELLS), f32),
            pltpu.VMEM((snaps, snaps, SHELLS), f32),
            pltpu.VMEM((x_n, snaps, SHELLS), f32),
            pltpu.VMEM((snaps, SHELLS), f32),
            pltpu.VMEM((z_hi_n, snaps, SHELLS), f32),
            pltpu.VMEM((snaps, 2, 2, SHELLS), f32),
            pltpu.VMEM((z_hi_n, snaps, 2, 2, SHELLS), f32),
            pltpu.VMEM((snaps, 1, SHELLS), f32),
            pltpu.VMEM((OUT_ROWS, SHELLS), f32),
            dma((4,)),
            dma((snaps,)),
            dma((CORES, snaps)),
            dma(()),
            dma(()),
            dma((snaps,)),
            dma((snaps,)),
            dma((x_n,)),
            dma((x_n,)),
            dma((heads, snaps)),
            dma((z_hi_n, snaps)),
            dma((3,)),
            dma(()),
        ],
        compiler_params=pltpu.CompilerParams(collective_id=0, has_side_effects=True),
    )(vel, ids, ref_order)
    return pl.pallas_call(
        functools.partial(finish, snaps),
        out_shape=(
            jax.ShapeDtypeStruct((1, snaps, SHELLS), f32),
            jax.ShapeDtypeStruct((1, SHELLS), f32),
        ),
        in_specs=[pl.BlockSpec(memory_space=pltpu.VMEM)],
        out_specs=(pl.BlockSpec(memory_space=pl.ANY),) * 2,
        scratch_shapes=[dma((2,))],
    )(pltpu.with_memory_space_constraint(done, pltpu.VMEM))


def solution(mesh):
    snaps, slabs = mesh.shape["tm"], mesh.shape["slab"]
    z_hi_n = min(Z_HI, slabs // CORES)
    sizes = (snaps, slabs // CORES // z_hi_n, z_hi_n)
    return jax.shard_map(
        functools.partial(body, sizes),
        mesh=mesh,
        in_specs=(P("tm", None, None, "slab"), P("slab"), P()),
        out_specs=(P("tm", None, None), P("tm", None)),
        check_vma=False,
    )
```

time: 115 us -> 40.1 us (0.35)
  blocking collectives: 64 us -> 0 us
  Pallas kernels: 0 us -> 39.4 us
  local copies, waits for them, and re-layouts: 16.7 us -> 0 us
  matrix products: 12.3 us -> 0 us
  waiting for transfers between devices: 10.7 us -> 0 us
  starting transfers between devices: 7.1 us -> 0 us
  other arithmetic: 2.63 us -> 0 us
    all_to_all x3 -> x0, blocking collectives: 64 us -> none  [the longest x1 35.2 us: copy_for_each(): lax.all_to_all(jnp.broadcast_to(array[None], (devices, *array.shape)), ax...]
    pallas_call x0 -> x2, Pallas kernels: none -> 39.4 us  [the longest x1 38.8 us: body(): pl.pallas_call(functools.partial(kernel, sizes), out_shape=pltpu.VMEM((sn...]
    dot_general x6 -> x0, matrix products: 12.3 us -> none  [the longest x1 5.98 us: body(): jnp.einsum('tcpm,rcpm->trm', rotated, local_modes, preferred_element_type...]
    all_to_all x2 -> x0, waiting for transfers between devices: 10.7 us -> none  [the longest x1 7.04 us: copy_for_each(): lax.all_to_all(jnp.broadcast_to(array[None], (devices, *array.shape)), ax...]
    dot_general x2 -> x0, local copies, waits for them, and re-layouts: 9.34 us -> none  [the longest x1 4.94 us: body(): jnp.einsum('tcpm,rcpm->trm', local_modes, local_modes, preferred_element_...]
    all_to_all x2 -> x0, starting transfers between devices: 7.1 us -> none  [the longest x1 3.63 us: turned_blocks(): whole = lax.all_to_all(whole, axes[k], k, k, tiled=True)]
    another operation x2 -> x0, local copies, waits for them, and re-layouts: 2.52 us -> none  [the longest x1 1.44 us: in_order(): parts.reshape(*shape[:dim], shape[dim] * shape[dim + 1], *shape[dim + 2:])]
    reshape x5 -> x0, local copies, waits for them, and re-layouts: 1.82 us -> none  [the longest x2 1.25 us: cut_along(): return jnp.moveaxis(array.reshape(*before, devices, -1, *after), dim, 0)]
  transfers between devices with their start and end apart: 2 -> 0, of which waited for: 2 -> 0; matrix products, arithmetic and copies ran while one was open for 1% -> 0% of each run, Pallas kernels for 0% -> 0%
where the time goes in v2:
time: 40.1 us; the launch traced here: 40 us
  Pallas kernels  39.4 us (98%)
  between operations  0.64 us (2%)
    pallas_call x1, Pallas kernels, body(): pl.pallas_call(functools.partial(kernel, sizes), out_shape=pltpu.VMEM((sn...  38.8 us

profile of v2, /device:TPU:1, one launch (start us, length us, event | category | flops | bytes accessed | tf_op | source)
XLA Modules:
  0.0 40.0 jit_solution(14662621099801352417)
XLA Ops:
  0.6 38.8 %shard_map.50.done_ref = f32[17,128]{1,0:T(8,128)S(1)} custom-call(bf16[3,256,128]{2,1,0:T(8,128)(2,1)} %bitcast.6, s32[128,128]{1,0:T(8,128)} %bitcast.7, s32[16]{0:T(128)} %order_hbm.1), custom_call_target="tpu_custom_call" | custom-call | tf_op jit(solution)/shard_map/pallas_call | solution.py:482
  39.4 0.6 %shard_map.51 = (f32[1,16,128]{2,1,0:T(8,128)}, f32[1,128]{1,0:T(1,128)}) custom-call(f32[17,128]{1,0:T(8,128)S(1)} %shard_map.50.done_ref), custom_call_target="tpu_custom_call" | custom-call | tf_op jit(solution)/shard_map/pallas_call | solution.py:520

commit v3 on v2

--- a/solution.py
+++ b/solution.py
@@ -25,6 +25,14 @@
         device_id={"tm": tm, "slab": slab},
         device_id_type=pl.DeviceIdType.MESH,
     )
+
+
+def arrived(ref, sem):
+    remote(ref, ref, sem, sem, lax.axis_index("tm"), lax.axis_index("slab")).wait_recv()
+
+
+def left(ref, sem):
+    remote(ref, ref, sem, sem, lax.axis_index("tm"), lax.axis_index("slab")).wait_send()
 
 
 def ordered_sum(terms):
@@ -47,6 +55,7 @@
     wide,
     terms,
     onehot,
+    binned,
     sums,
     r_recv,
     x_recv,
@@ -66,6 +75,7 @@
     x_send,
     x_rsem,
     p_send,
+    o_send,
     p_rsem,
     f_send,
     f_rsem,
@@ -90,6 +100,11 @@
     def slab_of(xx, zz, cc):
         return (xx * z_hi_n + zz) * CORES + cc
 
+    def many(n):
+        if 2 * n > vel_ref.shape[1]:
+            return vel_ref.at[pl.ds(0, 2), pl.ds(0, n)]
+        return vel_ref.at[0, pl.ds(0, 2 * n)]
+
     def rows_of(t, n):
         return pl.ds(pl.multiple_of(t * n, n), n)
 
@@ -99,9 +114,9 @@
         shell_ref.at[rows_of(me, GROUPS)], ids.at[core], load_sem.at[1]
     )
     load_own = pltpu.make_async_copy(
-        vel_ref.at[:, rows_of(me, ROWS)], recv.at[1, me], load_sem.at[2]
+        vel_ref.at[:, rows_of(me, ROWS)], recv.at[1, me], m_recv.at[1]
     )
-    load_order = pltpu.make_async_copy(order_hbm, order_ref, load_sem.at[3])
+    load_order = pltpu.make_async_copy(order_hbm, order_ref, load_sem.at[2])
 
     barrier = pltpu.get_barrier_semaphore()
 
@@ -154,14 +169,67 @@
         return remote(
             src.at[:, rows_of(there(d), ROWS)],
             recv.at[core, me],
-            m_send.at[d],
-            m_recv.at[core, d],
+            m_send,
+            m_recv.at[core],
             there(d),
             near,
         )
 
     def ids_copy():
         return remote(ids.at[0], ids.at[0], i_send, i_recv, me, near)
+
+    ahead = 1 if x_n > 1 else 0
+    first_head = (me == 0) & (z_hi == 0)
+    late = z_hi_n - 1 - z_hi
+
+    def forward(xx, zz, c):
+        remote(final, final, f_send, f_rsem, me, slab_of(xx, zz, c)).start()
+
+    def forward_all():
+        for xx in range(x_n):
+
+            @pl.when(x == xx)
+            def _(xx=xx):
+                if xx or not ahead:
+                    forward(xx, z_hi, 0)
+                else:
+
+                    @pl.when(jnp.logical_not(first_head))
+                    def _():
+                        forward(xx, z_hi, 0)
+
+                if xx == ahead and xx:
+
+                    @pl.when(first_head)
+                    def _():
+                        forward(0, z_hi, 0)
+
+                @pl.when(late >= heads)
+                def _():
+                    for to in {0: () if ahead else (0,), 1: (0, 1)}.get(xx, (xx,)):
+                        forward(to, late, 1)
+                        forward(to, late, 0)
+
+    def forwards_left():
+        for xx in range(x_n):
+            for is_first in (False, True):
+                for has_late in (False, True):
+                    copies = 1
+                    if xx == 0 and ahead and is_first:
+                        copies -= 1
+                    if xx == 1 and is_first:
+                        copies += 1
+                    if has_late:
+                        copies += 2 * len({0: () if ahead else (0,), 1: (0, 1)}.get(xx, (xx,)))
+                    if copies:
+
+                        @pl.when(
+                            (x == xx)
+                            & (first_head == is_first)
+                            & ((late >= heads) == has_late)
+                        )
+                        def _(copies=copies):
+                            left(many(copies * OUT_ROWS), f_send)
 
     load_all.wait()
     for d in by_distance:
@@ -193,46 +261,37 @@
                         at = (t + snaps) * PITCH
                         wide[c, at : at + ROWS, :] = value
 
-        def products():
-            for g in range(GROUPS):
-
-                def rows(c, p, d):
-                    return wide[c, pl.ds(d * PITCH + 2 * g + p, snaps, stride=PITCH), :]
-
-                def put(k, value):
-                    terms[k * snaps : (k + 1) * snaps, g * LANES : (g + 1) * LANES] = value.astype(
-                        jnp.bfloat16
-                    )
-
-                own = [[rows(c, p, 0) for p in range(2)] for c in range(3)]
-                put(0, sum(own[c][p] * own[c][p] for c in range(3) for p in range(2)))
-                for d in range(1, half + 1):
-                    other = [[rows(c, p, d) for p in range(2)] for c in range(3)]
-                    real = sum(own[c][p] * other[c][p] for c in range(3) for p in range(2))
-                    imag = sum(own[c][1] * other[c][0] - own[c][0] * other[c][1] for c in range(3))
-                    if d < half:
-                        put(2 * d - 1, real)
-                        put(2 * d, imag)
-                    else:
-                        put(2 * d - 1, jnp.where(first, real, imag))
-
-        def binned(c):
+        def products(g):
+            def rows(c, p, d):
+                return wide[c, pl.ds(d * PITCH + 2 * g + p, snaps, stride=PITCH), :]
+
+            def put(k, value):
+                terms[k * snaps : (k + 1) * snaps, g * LANES : (g + 1) * LANES] = value.astype(
+                    jnp.bfloat16
+                )
+
+            own = [[rows(c, p, 0) for p in range(2)] for c in range(3)]
+            put(0, sum(own[c][p] * own[c][p] for c in range(3) for p in range(2)))
+            for d in range(1, half + 1):
+                other = [[rows(c, p, d) for p in range(2)] for c in range(3)]
+                real = sum(own[c][p] * other[c][p] for c in range(3) for p in range(2))
+                imag = sum(own[c][1] * other[c][0] - own[c][0] * other[c][1] for c in range(3))
+                if d < half:
+                    put(2 * d - 1, real)
+                    put(2 * d, imag)
+                else:
+                    put(2 * d - 1, jnp.where(first, real, imag))
+
+        def bin_part(core_of, q):
+            for g in (2 * q, 2 * q + 1):
+                products(g)
+            modes = slice(2 * q * LANES, 2 * (q + 1) * LANES)
             return lax.dot_general(
-                terms[...],
-                onehot[c],
+                terms[:, modes],
+                onehot[core_of, :, modes],
                 (((1,), (1,)), ((), ())),
                 preferred_element_type=jnp.float32,
             )
-
-        def wait_part(c, d):
-            remote(
-                src.at[:, pl.ds(0, ROWS)],
-                recv.at[c, whence(d)],
-                m_send.at[d],
-                m_recv.at[c, d],
-                me,
-                slab,
-            ).wait_recv()
 
         with jax.named_scope("c_onehot"):
             load_ids.wait()
@@ -240,20 +299,19 @@
             ids_copy().wait_recv()
             spread_shells(0)
         with jax.named_scope("d_wait1"):
-            load_own.wait()
-            for d in reversed(by_distance):
-                wait_part(1, d)
+            arrived(recv.at[1], m_recv.at[1])
         with jax.named_scope("e_work1"):
             widen(1)
-            products()
-            sums[...] = binned(1)
+            binned[...] = bin_part(1, 0)
+            for q in range(1, GROUPS // 2):
+                binned[...] += bin_part(1, q)
         with jax.named_scope("f_wait0"):
-            for d in [0, *reversed(by_distance)]:
-                wait_part(0, d)
+            arrived(recv.at[0], m_recv.at[0])
         with jax.named_scope("g_work0"):
             widen(0)
-            products()
-            both = sums[...] + binned(0)
+            for q in range(GROUPS // 2 - 1):
+                binned[...] += bin_part(0, q)
+            both = binned[...] + bin_part(0, GROUPS // 2 - 1)
             for k in range(snaps):
                 sums[pl.ds(k, snaps, stride=snaps), :] = both[k * snaps : (k + 1) * snaps]
 
@@ -262,21 +320,13 @@
                 remote(
                     sums.at[rows_of(there(d), snaps)],
                     r_recv.at[me],
-                    r_send.at[d],
-                    r_rsem.at[d],
+                    r_send,
+                    r_rsem,
                     there(d),
                     slab,
                 ).start()
             r_recv[me] = sums[rows_of(me, snaps), :]
-            for d in reversed(by_distance):
-                remote(
-                    sums.at[pl.ds(0, snaps)],
-                    r_recv.at[whence(d)],
-                    r_send.at[d],
-                    r_rsem.at[d],
-                    me,
-                    slab,
-                ).wait_recv()
+            arrived(r_recv.at[pl.ds(0, snaps - 1)], r_rsem)
             x_recv[x] = ordered_sum([r_recv[t] for t in range(snaps)])
 
         with jax.named_scope("i_x"):
@@ -284,20 +334,13 @@
                 remote(
                     x_recv.at[x],
                     x_recv.at[x],
-                    x_send.at[d],
-                    x_rsem.at[d],
+                    x_send,
+                    x_rsem,
                     me,
                     slab_of((x + d) % x_n, z_hi, 1),
                 ).start()
-            for d in range(1, x_n):
-                remote(
-                    x_recv.at[x],
-                    x_recv.at[(x + x_n - d) % x_n],
-                    x_send.at[d],
-                    x_rsem.at[d],
-                    me,
-                    slab,
-                ).wait_recv()
+            if x_n > 1:
+                arrived(x_recv.at[pl.ds(0, x_n - 1)], x_rsem)
             total = ordered_sum([x_recv[i] for i in range(x_n)])
 
         with jax.named_scope("j_pairs"):
@@ -318,8 +361,8 @@
             return remote(
                 pair_ref(pair_src, d),
                 pair_ref(pair_recv.at[z_hi], d),
-                p_send.at[h, d],
-                p_rsem.at[z_hi, d],
+                p_send,
+                p_rsem,
                 there(d),
                 slab_of(x, h, 1),
             )
@@ -328,8 +371,8 @@
             return remote(
                 own_src,
                 own_recv.at[z_hi],
-                p_send.at[h, 0],
-                p_rsem.at[z_hi, 0],
+                o_send,
+                p_rsem,
                 me,
                 slab_of(x, h, 1),
             )
@@ -347,38 +390,11 @@
                 def _(h=h):
                     own_recv[h] = own_src[...]
 
-        def to_late(c):
-            return remote(
-                final,
-                final,
-                f_send.at[c],
-                f_rsem,
-                me,
-                slab_of(x, z_hi_n - 1 - z_hi, c),
-            )
-
-        def to_partner():
-            return remote(final, final, f_send.at[2], f_rsem, me, far)
-
         @pl.when(z_hi < heads)
         def _():
             with jax.named_scope("l_pairwait"):
-                for h in range(z_hi_n):
-                    for d in reversed(by_distance):
-                        remote(
-                            pair_ref(pair_src, d),
-                            pair_ref(pair_recv.at[h], d),
-                            p_send.at[0, d],
-                            p_rsem.at[h, d],
-                            me,
-                            slab,
-                        ).wait_recv()
-
-                    @pl.when(z_hi != h)
-                    def _(h=h):
-                        remote(
-                            own_src, own_recv.at[h], p_send.at[0, 0], p_rsem.at[h, 0], me, slab
-                        ).wait_recv()
+                each = 4 * half + 2 * (snaps - 1 - half)
+                arrived(many(z_hi_n * each + (z_hi_n - 1) * snaps), p_rsem)
 
             with jax.named_scope("m_coh"):
                 load_order.wait()
@@ -402,63 +418,43 @@
                     coh_rows[e] = (re * re + im * im) / (spec * energy[e])
                 for j in range(snaps):
                     final[j : j + 1, :] = coh_rows[(me - order_ref[j] + snaps) % snaps]
-                to_partner().start()
-
-                @pl.when(z_hi_n - 1 - z_hi >= heads)
-                def _():
-                    for c in (1, 0):
-                        to_late(c).start()
+                forward_all()
 
         @pl.when(z_hi >= heads)
         def _():
             with jax.named_scope("n_finalwait"):
-                remote(final, final, f_send.at[0], f_rsem, me, slab).wait_recv()
+                arrived(final, f_rsem)
                 load_order.wait()
 
     @pl.when(core == 0)
     def _():
         with jax.named_scope("n_finalwait"):
-            remote(final, final, f_send.at[0], f_rsem, me, slab).wait_recv()
+            arrived(final, f_rsem)
 
     with jax.named_scope("o_end"):
         out_ref[...] = final[0 : snaps + 1]
-        for d in by_distance:
-            part_copy(d).wait_send()
-
         @pl.when(core == 0)
         def _():
-            part_copy(0).wait_send()
-            ids_copy().wait_send()
+            left(src, m_send)
+            left(ids.at[0], i_send)
 
         @pl.when(core == 1)
         def _():
-            for d in range(1, snaps):
-                remote(
-                    sums.at[pl.ds(0, snaps)], r_recv.at[0], r_send.at[d], r_rsem.at[d], me, slab
-                ).wait_send()
-            for d in range(1, x_n):
-                remote(
-                    x_recv.at[x], x_recv.at[x], x_send.at[d], x_rsem.at[d], me, slab
-                ).wait_send()
-            for h in range(heads):
-                for d in range(1, snaps):
-                    ref = pair_src.at[d] if d <= half else pair_src.at[d, 0]
-                    remote(ref, ref, p_send.at[h, d], p_rsem.at[0, d], me, slab).wait_send()
-
-                @pl.when(z_hi != h)
-                def _(h=h):
-                    remote(
-                        own_src, own_src, p_send.at[h, 0], p_rsem.at[0, 0], me, slab
-                    ).wait_send()
+            left(recv.at[1, pl.ds(0, snaps - 1)], m_send)
+            left(r_recv.at[pl.ds(0, snaps - 1)], r_send)
+            if x_n > 1:
+                left(x_recv.at[pl.ds(0, x_n - 1)], x_send)
+            left(many(heads * (4 * half + 2 * (snaps - 1 - half))), p_send)
 
             @pl.when(z_hi < heads)
             def _():
-                remote(final, final, f_send.at[2], f_rsem, me, slab).wait_send()
-
-                @pl.when(z_hi_n - 1 - z_hi >= heads)
-                def _():
-                    for c in (1, 0):
-                        remote(final, final, f_send.at[c], f_rsem, me, slab).wait_send()
+                if heads > 1:
+                    left(own_recv.at[pl.ds(0, heads - 1)], o_send)
+                forwards_left()
+
+            @pl.when(z_hi >= heads)
+            def _():
+                left(own_recv.at[pl.ds(0, heads)], o_send)
 
 
 def finish(snaps, done_ref, coh_ref, spec_ref, sem):
@@ -493,6 +489,7 @@
             pltpu.VMEM((snaps * snaps, GROUPS * LANES), bf16),
             pltpu.VMEM((CORES, SHELLS, GROUPS * LANES), bf16),
             pltpu.VMEM((snaps * snaps, SHELLS), f32),
+            pltpu.VMEM((snaps * snaps, SHELLS), f32),
             pltpu.VMEM((snaps, snaps, SHELLS), f32),
             pltpu.VMEM((x_n, snaps, SHELLS), f32),
             pltpu.VMEM((snaps, SHELLS), f32),
@@ -501,19 +498,10 @@
             pltpu.VMEM((z_hi_n, snaps, 2, 2, SHELLS), f32),
             pltpu.VMEM((snaps, 1, SHELLS), f32),
             pltpu.VMEM((OUT_ROWS, SHELLS), f32),
-            dma((4,)),
-            dma((snaps,)),
-            dma((CORES, snaps)),
-            dma(()),
-            dma(()),
-            dma((snaps,)),
-            dma((snaps,)),
-            dma((x_n,)),
-            dma((x_n,)),
-            dma((heads, snaps)),
-            dma((z_hi_n, snaps)),
             dma((3,)),
             dma(()),
+            dma((CORES,)),
+            *[dma(())] * 11,
         ],
         compiler_params=pltpu.CompilerParams(collective_id=0, has_side_effects=True),
     )(vel, ids, ref_order)

time: 40.1 us -> 37.7 us (0.940)
  Pallas kernels: 39.4 us -> 36.9 us
    pallas_call x1, Pallas kernels: 38.8 us -> 36.3 us  [body(): pl.pallas_call(functools.partial(kernel, sizes), out_shape=pltpu.VMEM((sn...]
where the time goes in v3:
time: 37.7 us; the launch traced here: 37.5 us
  Pallas kernels  36.9 us (98%)
  between operations  0.64 us (2%)
    pallas_call x1, Pallas kernels, body(): pl.pallas_call(functools.partial(kernel, sizes), out_shape=pltpu.VMEM((sn...  36.3 us

profile of v3, /device:TPU:1, one launch (start us, length us, event | category | flops | bytes accessed | tf_op | source)
XLA Modules:
  0.0 37.5 jit_solution(4004775997063570790)
XLA Ops:
  0.6 36.3 %shard_map.50.done_ref = f32[17,128]{1,0:T(8,128)S(1)} custom-call(bf16[3,256,128]{2,1,0:T(8,128)(2,1)} %bitcast.6, s32[128,128]{1,0:T(8,128)} %bitcast.7, s32[16]{0:T(128)} %order_hbm.1), custom_call_target="tpu_custom_call" | custom-call | tf_op jit(solution)/shard_map/pallas_call | solution.py:478
  36.9 0.6 %shard_map.51 = (f32[1,16,128]{2,1,0:T(8,128)}, f32[1,128]{1,0:T(1,128)}) custom-call(f32[17,128]{1,0:T(8,128)S(1)} %shard_map.50.done_ref), custom_call_target="tpu_custom_call" | custom-call | tf_op jit(solution)/shard_map/pallas_call | solution.py:508

commit v4 on v3

--- a/solution.py
+++ b/solution.py
@@ -13,6 +13,8 @@
 ROWS = 16
 GROUPS = ROWS // 2
 PITCH = ROWS + 1
+HALVES = 2
+PIECE = ROWS // HALVES
 OUT_ROWS = 24
 
 
@@ -50,7 +52,8 @@
     out_ref,
     src,
     recv,
-    ids,
+    all_ids,
+    peer_ids,
     order_ref,
     wide,
     terms,
@@ -59,10 +62,15 @@
     sums,
     r_recv,
     x_recv,
+    spec_out,
+    spec_peer,
+    spec_x,
+    spec_recv,
     own_src,
     own_recv,
     pair_src,
     pair_recv,
+    spec_rows,
     coh_rows,
     final,
     load_sem,
@@ -75,8 +83,15 @@
     x_send,
     x_rsem,
     p_send,
+    p_rsem,
     o_send,
-    p_rsem,
+    o_rsem,
+    e_send,
+    e_rsem,
+    s_send,
+    s_rsem,
+    t_send,
+    t_rsem,
     f_send,
     f_rsem,
 ):
@@ -91,6 +106,15 @@
     near = far + 1
     by_distance = sorted(range(1, snaps), key=lambda d: (-min(d, snaps - d), d))
 
+    pairs_at = {0: (1,)}
+    for step in range(1, (half + 1) // 2 + 1):
+        pairs_at[step] = tuple(d for d in (2 * step - 1, 2 * step) if d <= half)
+    for step in range(1, half // 2 + 1):
+        pairs_at[-step] = tuple(d for d in (2 * step, 2 * step + 1) if d <= half)
+    steps = sorted((i for i in pairs_at if i), key=lambda i: (-abs(i), i))
+    x_steps = sorted(range(1, x_n), key=lambda d: -min(d, x_n - d))
+    pair_rows = sum(2 * len(pairs_at[i]) for i in steps)
+
     def there(d):
         return (me + d) % snaps
 
@@ -101,6 +125,8 @@
         return (xx * z_hi_n + zz) * CORES + cc
 
     def many(n):
+        if n <= r_recv.shape[1]:
+            return r_recv.at[0, pl.ds(0, n)]
         if 2 * n > vel_ref.shape[1]:
             return vel_ref.at[pl.ds(0, 2), pl.ds(0, n)]
         return vel_ref.at[0, pl.ds(0, 2 * n)]
@@ -110,12 +136,16 @@
 
     load_all = pltpu.make_async_copy(vel_ref, src, load_sem.at[0])
     load_all.start()
-    load_ids = pltpu.make_async_copy(
-        shell_ref.at[rows_of(me, GROUPS)], ids.at[core], load_sem.at[1]
-    )
-    load_own = pltpu.make_async_copy(
-        vel_ref.at[:, rows_of(me, ROWS)], recv.at[1, me], m_recv.at[1]
-    )
+    load_ids = pltpu.make_async_copy(shell_ref, all_ids, load_sem.at[1])
+    load_ids.start()
+    load_own = [
+        pltpu.make_async_copy(
+            vel_ref.at[:, pl.ds(pl.multiple_of(me * ROWS + n * PIECE, PIECE), PIECE)],
+            recv.at[1, n, me],
+            m_recv.at[1, n],
+        )
+        for n in range(HALVES)
+    ]
     load_order = pltpu.make_async_copy(order_hbm, order_ref, load_sem.at[2])
 
     barrier = pltpu.get_barrier_semaphore()
@@ -136,18 +166,17 @@
             for d in range(1, x_n):
                 greet(there(0), slab_of((x + d) % x_n, z_hi, 1))
 
-        load_ids.start()
-
         @pl.when(core == 1)
         def _():
-            load_own.start()
+            for copy in load_own:
+                copy.start()
             load_order.start()
 
             @pl.when(z_hi < heads)
             def _():
                 for h in range(1, z_hi_n):
-                    for d in range(snaps):
-                        greet(there(d), slab_of(x, (z_hi + h) % z_hi_n, 1))
+                    for i in pairs_at:
+                        greet((me + snaps - i) % snaps, slab_of(x, (z_hi + h) % z_hi_n, 1))
 
     with jax.named_scope("b_barrier"):
 
@@ -159,24 +188,57 @@
         def _():
             @pl.when(z_hi < heads)
             def _():
-                pl.semaphore_wait(barrier, snaps - 1 + x_n - 1 + (heads - 1) * snaps)
+                pl.semaphore_wait(barrier, snaps - 1 + x_n - 1 + (heads - 1) * len(pairs_at))
 
             @pl.when(z_hi >= heads)
             def _():
-                pl.semaphore_wait(barrier, snaps - 1 + x_n - 1 + heads * snaps)
-
-    def part_copy(d):
+                pl.semaphore_wait(barrier, snaps - 1 + x_n - 1 + heads * len(pairs_at))
+
+    def part_copy(n, d):
         return remote(
-            src.at[:, rows_of(there(d), ROWS)],
-            recv.at[core, me],
+            src.at[:, pl.ds(pl.multiple_of(there(d) * ROWS + n * PIECE, PIECE), PIECE)],
+            recv.at[core, n, me],
             m_send,
-            m_recv.at[core],
+            m_recv.at[core, n],
             there(d),
             near,
         )
 
     def ids_copy():
-        return remote(ids.at[0], ids.at[0], i_send, i_recv, me, near)
+        return remote(all_ids.at[rows_of(me, GROUPS)], peer_ids, i_send, i_recv, me, near)
+
+    def spec_copy():
+        return remote(spec_out, spec_peer, e_send, e_rsem, me, near)
+
+    shells = lax.broadcasted_iota(jnp.int32, (SHELLS, LANES), 0)
+
+    def local_spectrum():
+        lanes_n = shell_ref.shape[0]
+        squares = ordered_sum([src[c].astype(jnp.float32) ** 2 for c in range(3)])
+        wide[0, 0 : 2 * lanes_n, :] = squares
+        energy = wide[0, pl.ds(0, lanes_n, stride=2), :] + wide[0, pl.ds(1, lanes_n, stride=2), :]
+        wide[1, 0:lanes_n, :] = energy.astype(jnp.bfloat16).astype(jnp.float32)
+
+        def add_rows(i, total):
+            at = rows_of(i, 8)
+            shell, value = all_ids[at, :], wide[1, at, :]
+            for r in range(8):
+                hit = jnp.broadcast_to(shell[r : r + 1], (SHELLS, LANES)) == shells
+                total = total + jnp.where(
+                    hit, jnp.broadcast_to(value[r : r + 1], (SHELLS, LANES)), 0.0
+                )
+            return total
+
+        by_lane = lax.fori_loop(
+            0, lanes_n // 8, add_rows, jnp.zeros((SHELLS, LANES), jnp.float32)
+        )
+        return lax.dot_general(
+            jnp.ones((8, LANES), jnp.float32),
+            by_lane,
+            (((1,), (1,)), ((), ())),
+            precision=lax.Precision.HIGHEST,
+            preferred_element_type=jnp.float32,
+        )[0:1]
 
     ahead = 1 if x_n > 1 else 0
     first_head = (me == 0) & (z_hi == 0)
@@ -232,34 +294,39 @@
                             left(many(copies * OUT_ROWS), f_send)
 
     load_all.wait()
-    for d in by_distance:
-        part_copy(d).start()
 
     @pl.when(core == 0)
     def _():
-        part_copy(0).start()
+        for n in range(HALVES):
+            for d in [*by_distance, 0]:
+                part_copy(n, d).start()
         load_ids.wait()
         ids_copy().start()
+        spec_out[...] = local_spectrum()
+        spec_copy().start()
 
     @pl.when(core == 1)
     def _():
-        shells = lax.broadcasted_iota(jnp.int32, (SHELLS, LANES), 0)
+        for n in range(HALVES):
+            for d in by_distance:
+                part_copy(n, d).start()
+
         first = lax.broadcasted_iota(jnp.int32, (snaps, LANES), 0) < half
 
         def spread_shells(c):
             for g in range(GROUPS):
-                row = jnp.broadcast_to(ids[c, g : g + 1, :], (SHELLS, LANES))
+                row = all_ids[pl.ds(me * GROUPS + g, 1), :] if c else peer_ids[g : g + 1, :]
+                row = jnp.broadcast_to(row, (SHELLS, LANES))
                 hot = jnp.where(row == shells, 1.0, 0.0).astype(jnp.bfloat16)
                 onehot[c, :, g * LANES : (g + 1) * LANES] = hot
 
-        def widen(core_of):
+        def widen(core_of, n):
             for t in range(snaps):
                 for c in range(3):
-                    value = recv[core_of, t, c].astype(jnp.float32)
-                    wide[c, t * PITCH : t * PITCH + ROWS, :] = value
-                    if t < half:
-                        at = (t + snaps) * PITCH
-                        wide[c, at : at + ROWS, :] = value
+                    value = recv[core_of, n, t, c].astype(jnp.float32)
+                    for at in (t, t + snaps) if t < half else (t,):
+                        row = at * PITCH + n * PIECE
+                        wide[c, row : row + PIECE, :] = value
 
         def products(g):
             def rows(c, p, d):
@@ -271,16 +338,15 @@
                 )
 
             own = [[rows(c, p, 0) for p in range(2)] for c in range(3)]
-            put(0, sum(own[c][p] * own[c][p] for c in range(3) for p in range(2)))
             for d in range(1, half + 1):
                 other = [[rows(c, p, d) for p in range(2)] for c in range(3)]
                 real = sum(own[c][p] * other[c][p] for c in range(3) for p in range(2))
                 imag = sum(own[c][1] * other[c][0] - own[c][0] * other[c][1] for c in range(3))
                 if d < half:
-                    put(2 * d - 1, real)
-                    put(2 * d, imag)
+                    put(2 * d - 2, real)
+                    put(2 * d - 1, imag)
                 else:
-                    put(2 * d - 1, jnp.where(first, real, imag))
+                    put(2 * d - 2, jnp.where(first, real, imag))
 
         def bin_part(core_of, q):
             for g in (2 * q, 2 * q + 1):
@@ -298,22 +364,43 @@
             spread_shells(1)
             ids_copy().wait_recv()
             spread_shells(0)
-        with jax.named_scope("d_wait1"):
-            arrived(recv.at[1], m_recv.at[1])
-        with jax.named_scope("e_work1"):
-            widen(1)
-            binned[...] = bin_part(1, 0)
-            for q in range(1, GROUPS // 2):
-                binned[...] += bin_part(1, q)
-        with jax.named_scope("f_wait0"):
-            arrived(recv.at[0], m_recv.at[0])
-        with jax.named_scope("g_work0"):
-            widen(0)
-            for q in range(GROUPS // 2 - 1):
-                binned[...] += bin_part(0, q)
-            both = binned[...] + bin_part(0, GROUPS // 2 - 1)
-            for k in range(snaps):
-                sums[pl.ds(k, snaps, stride=snaps), :] = both[k * snaps : (k + 1) * snaps]
+        with jax.named_scope("c_spectrum"):
+            mine = local_spectrum()
+            spec_copy().wait_recv()
+            spec_x[x] = mine + spec_peer[...]
+            for d in x_steps:
+                remote(
+                    spec_x.at[x],
+                    spec_x.at[x],
+                    t_send,
+                    t_rsem,
+                    me,
+                    slab_of((x + d) % x_n, z_hi, 1),
+                ).start()
+
+        quarters = GROUPS // 2 // HALVES
+        for n in range(HALVES):
+            for c in (1, 0):
+                with jax.named_scope(f"d_wait{n}{c}"):
+                    arrived(recv.at[c, n], m_recv.at[c, n])
+                with jax.named_scope(f"e_work{n}{c}"):
+                    widen(c, n)
+                    for q in range(n * quarters, (n + 1) * quarters):
+                        if (n, c) == (HALVES - 1, 0) and q == (n + 1) * quarters - 1:
+                            both = binned[...] + bin_part(c, q)
+                        elif (n, c, q) == (0, 1, 0):
+                            binned[...] = bin_part(c, q)
+                        else:
+                            binned[...] += bin_part(c, q)
+        with jax.named_scope("g_turn"):
+            for k in range(snaps - 1):
+                value, shift = both[k * snaps : (k + 1) * snaps], (k // 2 + 1) // 2
+                sums[pl.ds(shift * snaps + k, snaps - shift, stride=snaps), :] = value[
+                    0 : snaps - shift
+                ]
+                if shift:
+                    sums[pl.ds(k, shift, stride=snaps), :] = value[snaps - shift :]
+            sums[pl.ds(snaps - 1, snaps, stride=snaps), :] = jnp.zeros((snaps, SHELLS), jnp.float32)
 
         with jax.named_scope("h_owner"):
             for d in by_distance:
@@ -326,11 +413,18 @@
                     slab,
                 ).start()
             r_recv[me] = sums[rows_of(me, snaps), :]
+            if x_n > 1:
+                arrived(spec_x.at[pl.ds(0, x_n - 1)], t_rsem)
+            spec_recv[me] = ordered_sum([spec_x[i] for i in range(x_n)])
+            for d in by_distance:
+                remote(
+                    spec_recv.at[me], spec_recv.at[me], s_send, s_rsem, there(d), slab
+                ).start()
             arrived(r_recv.at[pl.ds(0, snaps - 1)], r_rsem)
             x_recv[x] = ordered_sum([r_recv[t] for t in range(snaps)])
 
         with jax.named_scope("i_x"):
-            for d in range(1, x_n):
+            for d in x_steps:
                 remote(
                     x_recv.at[x],
                     x_recv.at[x],
@@ -342,49 +436,33 @@
             if x_n > 1:
                 arrived(x_recv.at[pl.ds(0, x_n - 1)], x_rsem)
             total = ordered_sum([x_recv[i] for i in range(x_n)])
+            arrived(spec_recv.at[pl.ds(0, snaps - 1)], s_rsem)
 
         with jax.named_scope("j_pairs"):
-            own_src[...] = total
-            for d in range(1, snaps):
-                pair_src[d, 0, 0:1, :] = total[0:1]
-                if d < half:
-                    pair_src[d, 1, :, :] = total[2 * d - 1 : 2 * d + 1]
-                elif d == half:
-                    pair_src[d, 1, 0:1, :] = total[2 * d - 1 : 2 * d]
-                    pair_src[d, 1, 1:2, :] = jnp.zeros((1, SHELLS), jnp.float32)
-                pair_src[d, 0, 1:2, :] = jnp.zeros((1, SHELLS), jnp.float32)
-
-        def pair_ref(ref, d):
-            return ref.at[d] if d <= half else ref.at[d, 0]
-
-        def pair_send(h, d):
-            return remote(
-                pair_ref(pair_src, d),
-                pair_ref(pair_recv.at[z_hi], d),
-                p_send,
-                p_rsem,
-                there(d),
-                slab_of(x, h, 1),
-            )
-
-        def own_send(h):
-            return remote(
-                own_src,
-                own_recv.at[z_hi],
-                o_send,
-                p_rsem,
-                me,
-                slab_of(x, h, 1),
-            )
+            own_src[0:snaps, :] = total
+            for t in range(snaps):
+                own_src[snaps + t : snaps + t + 1, :] = spec_recv[t]
+            for d in range(1, half + 1):
+                pair_src[d - 1] = total[2 * d - 2 : 2 * d]
 
         with jax.named_scope("k_send"):
             for h in range(heads):
-                for d in by_distance:
-                    pair_send(h, d).start()
+                for i in steps:
+                    count = len(pairs_at[i])
+                    remote(
+                        pair_src.at[pl.ds(pairs_at[i][0] - 1, count)],
+                        pair_recv.at[z_hi, steps.index(i), pl.ds(0, count)],
+                        p_send,
+                        p_rsem,
+                        (me + snaps + i) % snaps,
+                        slab_of(x, h, 1),
+                    ).start()
 
                 @pl.when(z_hi != h)
                 def _(h=h):
-                    own_send(h).start()
+                    remote(
+                        own_src, own_recv.at[z_hi], o_send, o_rsem, me, slab_of(x, h, 1)
+                    ).start()
 
                 @pl.when(z_hi == h)
                 def _(h=h):
@@ -393,29 +471,41 @@
         @pl.when(z_hi < heads)
         def _():
             with jax.named_scope("l_pairwait"):
-                each = 4 * half + 2 * (snaps - 1 - half)
-                arrived(many(z_hi_n * each + (z_hi_n - 1) * snaps), p_rsem)
+                arrived(many(z_hi_n * pair_rows), p_rsem)
+                if z_hi_n > 1:
+                    arrived(own_recv.at[pl.ds(0, z_hi_n - 1)], o_rsem)
 
             with jax.named_scope("m_coh"):
                 load_order.wait()
                 own = ordered_sum([own_recv[h] for h in range(z_hi_n)])
-                spec = own[0:1]
-                energy = [spec] + [
-                    ordered_sum([pair_recv[h, d, 0, 0:1, :] for h in range(z_hi_n)])
-                    for d in range(1, snaps)
-                ]
+                energy = own[snaps : 2 * snaps]
+                for t in range(snaps):
+                    spec_rows[t] = energy[t : t + 1]
+                spec = spec_rows[me]
                 final[snaps : snaps + 1, :] = spec
-                coh_rows[0] = spec * spec / (spec * spec)
-                for e in range(1, snaps):
-                    if e <= half:
-                        pair = ordered_sum([pair_recv[h, e, 1] for h in range(z_hi_n)])
-                        re, im = pair[0:1], pair[1:2]
-                        if e == half:
-                            im = own[2 * e - 1 : 2 * e]
-                    else:
-                        d = snaps - e
-                        re, im = own[2 * d - 1 : 2 * d], own[2 * d : 2 * d + 1]
-                    coh_rows[e] = (re * re + im * im) / (spec * energy[e])
+
+                def pair(i, d):
+                    if i == 0:
+                        return own[2 * d - 2 : 2 * d]
+                    at = pairs_at[i].index(d)
+                    return ordered_sum(
+                        [pair_recv[h, steps.index(i), at] for h in range(z_hi_n)]
+                    )
+
+                def power(rows):
+                    re, im = rows[0:1], rows[1:2]
+                    return re * re + im * im
+
+                def put_row(e, value):
+                    coh_rows[e] = value / (spec * spec_rows[(me + snaps - e) % snaps])
+
+                put_row(0, spec * spec)
+                for d in range(1, half):
+                    put_row(d, power(pair((d + 1) // 2, d)))
+                    put_row(snaps - d, power(pair(-(d // 2), d)))
+                re = pair((half + 1) // 2, half)[0:1]
+                im = pair(-(half // 2), half)[0:1]
+                put_row(half, re * re + im * im)
                 for j in range(snaps):
                     final[j : j + 1, :] = coh_rows[(me - order_ref[j] + snaps) % snaps]
                 forward_all()
@@ -436,15 +526,18 @@
         @pl.when(core == 0)
         def _():
             left(src, m_send)
-            left(ids.at[0], i_send)
+            left(peer_ids, i_send)
+            left(spec_out, e_send)
 
         @pl.when(core == 1)
         def _():
-            left(recv.at[1, pl.ds(0, snaps - 1)], m_send)
+            left(src.at[:, pl.ds(0, (snaps - 1) * ROWS)], m_send)
             left(r_recv.at[pl.ds(0, snaps - 1)], r_send)
             if x_n > 1:
                 left(x_recv.at[pl.ds(0, x_n - 1)], x_send)
-            left(many(heads * (4 * half + 2 * (snaps - 1 - half))), p_send)
+                left(spec_x.at[pl.ds(0, x_n - 1)], t_send)
+            left(spec_recv.at[pl.ds(0, snaps - 1)], s_send)
+            left(many(heads * pair_rows), p_send)
 
             @pl.when(z_hi < heads)
             def _():
@@ -482,26 +575,32 @@
         out_specs=pl.BlockSpec(memory_space=pltpu.VMEM),
         scratch_shapes=[
             pltpu.VMEM((3, 2 * lanes_n, LANES), bf16),
-            pltpu.VMEM((CORES, snaps, 3, ROWS, LANES), bf16),
-            pltpu.VMEM((CORES, GROUPS, LANES), jnp.int32),
+            pltpu.VMEM((CORES, HALVES, snaps, 3, PIECE, LANES), bf16),
+            pltpu.VMEM((lanes_n, LANES), jnp.int32),
+            pltpu.VMEM((GROUPS, LANES), jnp.int32),
             pltpu.SMEM((snaps,), jnp.int32),
             pltpu.VMEM((3, (snaps + half + 1) * PITCH, LANES), f32),
-            pltpu.VMEM((snaps * snaps, GROUPS * LANES), bf16),
+            pltpu.VMEM(((snaps - 1) * snaps, GROUPS * LANES), bf16),
             pltpu.VMEM((CORES, SHELLS, GROUPS * LANES), bf16),
-            pltpu.VMEM((snaps * snaps, SHELLS), f32),
+            pltpu.VMEM(((snaps - 1) * snaps, SHELLS), f32),
             pltpu.VMEM((snaps * snaps, SHELLS), f32),
             pltpu.VMEM((snaps, snaps, SHELLS), f32),
             pltpu.VMEM((x_n, snaps, SHELLS), f32),
-            pltpu.VMEM((snaps, SHELLS), f32),
-            pltpu.VMEM((z_hi_n, snaps, SHELLS), f32),
-            pltpu.VMEM((snaps, 2, 2, SHELLS), f32),
-            pltpu.VMEM((z_hi_n, snaps, 2, 2, SHELLS), f32),
+            pltpu.VMEM((1, SHELLS), f32),
+            pltpu.VMEM((1, SHELLS), f32),
+            pltpu.VMEM((x_n, 1, SHELLS), f32),
+            pltpu.VMEM((snaps, 1, SHELLS), f32),
+            pltpu.VMEM((2 * snaps, SHELLS), f32),
+            pltpu.VMEM((z_hi_n, 2 * snaps, SHELLS), f32),
+            pltpu.VMEM((half, 2, SHELLS), f32),
+            pltpu.VMEM((z_hi_n, half, 2, 2, SHELLS), f32),
+            pltpu.VMEM((snaps, 1, SHELLS), f32),
             pltpu.VMEM((snaps, 1, SHELLS), f32),
             pltpu.VMEM((OUT_ROWS, SHELLS), f32),
             dma((3,)),
             dma(()),
-            dma((CORES,)),
-            *[dma(())] * 11,
+            dma((CORES, HALVES)),
+            *[dma(())] * 18,
         ],
         compiler_params=pltpu.CompilerParams(collective_id=0, has_side_effects=True),
     )(vel, ids, ref_order)

time: 37.7 us -> 36.4 us (0.966)
  Pallas kernels: 36.9 us -> 35.6 us
    pallas_call x1, Pallas kernels: 36.3 us -> 35 us  [body(): pl.pallas_call(functools.partial(kernel, sizes), out_shape=pltpu.VMEM((sn...]
where the time goes in v4:
time: 36.4 us; the launch traced here: 36.3 us
  Pallas kernels  35.6 us (98%)
  between operations  0.64 us (2%)
    pallas_call x1, Pallas kernels, body(): pl.pallas_call(functools.partial(kernel, sizes), out_shape=pltpu.VMEM((sn...  35 us

profile of v4, /device:TPU:1, one launch (start us, length us, event | category | flops | bytes accessed | tf_op | source)
XLA Modules:
  0.0 36.3 jit_solution(10755448269010166313)
XLA Ops:
  0.6 35.0 %shard_map.50.done_ref = f32[17,128]{1,0:T(8,128)S(1)} custom-call(bf16[3,256,128]{2,1,0:T(8,128)(2,1)} %bitcast.6, s32[128,128]{1,0:T(8,128)} %bitcast.7, s32[16]{0:T(128)} %order_hbm.1), custom_call_target="tpu_custom_call" | custom-call | tf_op jit(solution)/shard_map/pallas_call | solution.py:571
  35.6 0.6 %shard_map.51 = (f32[1,16,128]{2,1,0:T(8,128)}, f32[1,128]{1,0:T(1,128)}) custom-call(f32[17,128]{1,0:T(8,128)S(1)} %shard_map.50.done_ref), custom_call_target="tpu_custom_call" | custom-call | tf_op jit(solution)/shard_map/pallas_call | solution.py:607

commit v5 on v4

--- a/solution.py
+++ b/solution.py
@@ -13,6 +13,7 @@
 ROWS = 16
 GROUPS = ROWS // 2
 PITCH = ROWS + 1
+SETS = 3
 HALVES = 2
 PIECE = ROWS // HALVES
 OUT_ROWS = 24
@@ -104,6 +105,9 @@
     x, z_hi = slab // CORES // z_hi_n, slab // CORES % z_hi_n
     far = slab - core
     near = far + 1
+    late = z_hi_n - 1 - z_hi
+    is_late = z_hi // heads
+    part_set = core + (1 - core) * 2 * is_late
     by_distance = sorted(range(1, snaps), key=lambda d: (-min(d, snaps - d), d))
 
     pairs_at = {0: (1,)}
@@ -159,9 +163,22 @@
 
         @pl.when(core == 1)
         def _():
-            for d in by_distance:
-                greet(there(d), near)
-                greet(there(d), far)
+            @pl.when(z_hi < heads)
+            def _():
+                @pl.when(late >= heads)
+                def _():
+                    for d in [*by_distance, 0]:
+                        greet(there(d), slab_of(x, late, 0))
+
+                for d in by_distance:
+                    greet(there(d), near)
+                    greet(there(d), far)
+
+            @pl.when(z_hi >= heads)
+            def _():
+                for d in by_distance:
+                    greet(there(d), near)
+
             greet(me, far)
             for d in range(1, x_n):
                 greet(there(0), slab_of((x + d) % x_n, z_hi, 1))
@@ -182,7 +199,13 @@
 
         @pl.when(core == 0)
         def _():
-            pl.semaphore_wait(barrier, snaps)
+            @pl.when(z_hi < heads)
+            def _():
+                pl.semaphore_wait(barrier, snaps)
+
+            @pl.when(z_hi >= heads)
+            def _():
+                pl.semaphore_wait(barrier, snaps + 1)
 
         @pl.when(core == 1)
         def _():
@@ -197,15 +220,22 @@
     def part_copy(n, d):
         return remote(
             src.at[:, pl.ds(pl.multiple_of(there(d) * ROWS + n * PIECE, PIECE), PIECE)],
-            recv.at[core, n, me],
+            recv.at[part_set, n, me],
             m_send,
-            m_recv.at[core, n],
+            m_recv.at[part_set, n],
             there(d),
-            near,
+            slab_of(x, z_hi + (1 - core) * is_late * (late - z_hi), 1),
         )
 
     def ids_copy():
-        return remote(all_ids.at[rows_of(me, GROUPS)], peer_ids, i_send, i_recv, me, near)
+        return remote(
+            all_ids.at[rows_of(me, GROUPS)],
+            peer_ids.at[is_late],
+            i_send,
+            i_recv.at[is_late],
+            me,
+            slab_of(x, z_hi + is_late * (late - z_hi), 1),
+        )
 
     def spec_copy():
         return remote(spec_out, spec_peer, e_send, e_rsem, me, near)
@@ -242,7 +272,6 @@
 
     ahead = 1 if x_n > 1 else 0
     first_head = (me == 0) & (z_hi == 0)
-    late = z_hi_n - 1 - z_hi
 
     def forward(xx, zz, c):
         remote(final, final, f_send, f_rsem, me, slab_of(xx, zz, c)).start()
@@ -315,7 +344,10 @@
 
         def spread_shells(c):
             for g in range(GROUPS):
-                row = all_ids[pl.ds(me * GROUPS + g, 1), :] if c else peer_ids[g : g + 1, :]
+                if c == 1:
+                    row = all_ids[pl.ds(me * GROUPS + g, 1), :]
+                else:
+                    row = peer_ids[c // 2, g : g + 1, :]
                 row = jnp.broadcast_to(row, (SHELLS, LANES))
                 hot = jnp.where(row == shells, 1.0, 0.0).astype(jnp.bfloat16)
                 onehot[c, :, g * LANES : (g + 1) * LANES] = hot
@@ -362,8 +394,12 @@
         with jax.named_scope("c_onehot"):
             load_ids.wait()
             spread_shells(1)
-            ids_copy().wait_recv()
-            spread_shells(0)
+
+            @pl.when(z_hi < heads)
+            def _():
+                arrived(peer_ids.at[0], i_recv.at[0])
+                spread_shells(0)
+
         with jax.named_scope("c_spectrum"):
             mine = local_spectrum()
             spec_copy().wait_recv()
@@ -379,22 +415,35 @@
                 ).start()
 
         quarters = GROUPS // 2 // HALVES
+
+        def work_off(c, n):
+            with jax.named_scope(f"d_wait{c}{n}"):
+                arrived(recv.at[c, n], m_recv.at[c, n])
+            with jax.named_scope(f"e_work{c}{n}"):
+                widen(c, n)
+                for q in range(n * quarters, (n + 1) * quarters):
+                    if (c, q) == (1, 0):
+                        binned[...] = bin_part(c, q)
+                    else:
+                        binned[...] += bin_part(c, q)
+
         for n in range(HALVES):
-            for c in (1, 0):
-                with jax.named_scope(f"d_wait{n}{c}"):
-                    arrived(recv.at[c, n], m_recv.at[c, n])
-                with jax.named_scope(f"e_work{n}{c}"):
-                    widen(c, n)
-                    for q in range(n * quarters, (n + 1) * quarters):
-                        if (n, c) == (HALVES - 1, 0) and q == (n + 1) * quarters - 1:
-                            both = binned[...] + bin_part(c, q)
-                        elif (n, c, q) == (0, 1, 0):
-                            binned[...] = bin_part(c, q)
-                        else:
-                            binned[...] += bin_part(c, q)
+            work_off(1, n)
+
+            @pl.when(z_hi < heads)
+            def _(n=n):
+                work_off(0, n)
+
+        @pl.when((z_hi < heads) & (late >= heads))
+        def _():
+            arrived(peer_ids.at[1], i_recv.at[1])
+            spread_shells(2)
+            for n in range(HALVES):
+                work_off(2, n)
+
         with jax.named_scope("g_turn"):
             for k in range(snaps - 1):
-                value, shift = both[k * snaps : (k + 1) * snaps], (k // 2 + 1) // 2
+                value, shift = binned[k * snaps : (k + 1) * snaps], (k // 2 + 1) // 2
                 sums[pl.ds(shift * snaps + k, snaps - shift, stride=snaps), :] = value[
                     0 : snaps - shift
                 ]
@@ -526,7 +575,7 @@
         @pl.when(core == 0)
         def _():
             left(src, m_send)
-            left(peer_ids, i_send)
+            left(peer_ids.at[0], i_send)
             left(spec_out, e_send)
 
         @pl.when(core == 1)
@@ -575,13 +624,13 @@
         out_specs=pl.BlockSpec(memory_space=pltpu.VMEM),
         scratch_shapes=[
             pltpu.VMEM((3, 2 * lanes_n, LANES), bf16),
-            pltpu.VMEM((CORES, HALVES, snaps, 3, PIECE, LANES), bf16),
+            pltpu.VMEM((SETS, HALVES, snaps, 3, PIECE, LANES), bf16),
             pltpu.VMEM((lanes_n, LANES), jnp.int32),
-            pltpu.VMEM((GROUPS, LANES), jnp.int32),
+            pltpu.VMEM((2, GROUPS, LANES), jnp.int32),
             pltpu.SMEM((snaps,), jnp.int32),
             pltpu.VMEM((3, (snaps + half + 1) * PITCH, LANES), f32),
             pltpu.VMEM(((snaps - 1) * snaps, GROUPS * LANES), bf16),
-            pltpu.VMEM((CORES, SHELLS, GROUPS * LANES), bf16),
+            pltpu.VMEM((SETS, SHELLS, GROUPS * LANES), bf16),
             pltpu.VMEM(((snaps - 1) * snaps, SHELLS), f32),
             pltpu.VMEM((snaps * snaps, SHELLS), f32),
             pltpu.VMEM((snaps, snaps, SHELLS), f32),
@@ -599,8 +648,10 @@
             pltpu.VMEM((OUT_ROWS, SHELLS), f32),
             dma((3,)),
             dma(()),
-            dma((CORES, HALVES)),
-            *[dma(())] * 18,
+            dma((SETS, HALVES)),
+            dma(()),
+            dma((2,)),
+            *[dma(())] * 16,
         ],
         compiler_params=pltpu.CompilerParams(collective_id=0, has_side_effects=True),
     )(vel, ids, ref_order)

time: 36.4 us -> 36.2 us (level)
  no operation moved by 1% of the time
where the time goes in v5:
time: 36.2 us; the launch traced here: 36.1 us
  Pallas kernels  35.4 us (98%)
  between operations  0.64 us (2%)
    pallas_call x1, Pallas kernels, body(): pl.pallas_call(functools.partial(kernel, sizes), out_shape=pltpu.VMEM((sn...  34.8 us

profile of v5, /device:TPU:1, one launch (start us, length us, event | category | flops | bytes accessed | tf_op | source)
XLA Modules:
  0.0 36.1 jit_solution(6334386753248790616)
XLA Ops:
  0.6 34.8 %shard_map.50.done_ref = f32[17,128]{1,0:T(8,128)S(1)} custom-call(bf16[3,256,128]{2,1,0:T(8,128)(2,1)} %bitcast.6, s32[128,128]{1,0:T(8,128)} %bitcast.7, s32[16]{0:T(128)} %order_hbm.1), custom_call_target="tpu_custom_call" | custom-call | tf_op jit(solution)/shard_map/pallas_call | solution.py:620
  35.4 0.6 %shard_map.51 = (f32[1,16,128]{2,1,0:T(8,128)}, f32[1,128]{1,0:T(1,128)}) custom-call(f32[17,128]{1,0:T(8,128)S(1)} %shard_map.50.done_ref), custom_call_target="tpu_custom_call" | custom-call | tf_op jit(solution)/shard_map/pallas_call | solution.py:658

commit v6 on v5

--- a/solution.py
+++ b/solution.py
@@ -85,6 +85,8 @@
     x_rsem,
     p_send,
     p_rsem,
+    h_send,
+    h_rsem,
     o_send,
     o_rsem,
     e_send,
@@ -103,6 +105,11 @@
     slab = lax.axis_index("slab")
     core = slab % CORES
     x, z_hi = slab // CORES // z_hi_n, slab // CORES % z_hi_n
+    y_n, z_n = snaps // Z_LO, z_hi_n * Z_LO
+    y, z_lo = me // Z_LO, me % Z_LO
+    z = z_hi * Z_LO + z_lo
+    base = y * Z_LO
+    block = Z_LO * snaps
     far = slab - core
     near = far + 1
     late = z_hi_n - 1 - z_hi
@@ -115,9 +122,16 @@
         pairs_at[step] = tuple(d for d in (2 * step - 1, 2 * step) if d <= half)
     for step in range(1, half // 2 + 1):
         pairs_at[-step] = tuple(d for d in (2 * step, 2 * step + 1) if d <= half)
-    steps = sorted((i for i in pairs_at if i), key=lambda i: (-abs(i), i))
+    y_steps = sorted(range(1, y_n), key=lambda d: -min(d, y_n - d))
     x_steps = sorted(range(1, x_n), key=lambda d: -min(d, x_n - d))
-    pair_rows = sum(2 * len(pairs_at[i]) for i in steps)
+    messages = sorted(
+        ((k, i) for k in range(Z_LO) for i in pairs_at), key=lambda m: (-abs(m[1]), m)
+    )
+    away = [(k, i) for k, i in messages if not 0 <= k + i < Z_LO]
+    at_home = [(k, i) for k, i in messages if 0 <= k + i < Z_LO]
+    away_rows = sum(2 * len(pairs_at[i]) for _, i in away)
+    reach = sorted({k + i for k, i in messages})
+    slots = list(pairs_at)
 
     def there(d):
         return (me + d) % snaps
@@ -134,6 +148,9 @@
         if 2 * n > vel_ref.shape[1]:
             return vel_ref.at[pl.ds(0, 2), pl.ds(0, n)]
         return vel_ref.at[0, pl.ds(0, 2 * n)]
+
+    def home_rows(n):
+        return pair_recv.at[pl.ds(0, n), pl.ds(0, 3), 0]
 
     def rows_of(t, n):
         return pl.ds(pl.multiple_of(t * n, n), n)
@@ -192,8 +209,8 @@
             @pl.when(z_hi < heads)
             def _():
                 for h in range(1, z_hi_n):
-                    for i in pairs_at:
-                        greet((me + snaps - i) % snaps, slab_of(x, (z_hi + h) % z_hi_n, 1))
+                    for i in reach:
+                        greet((base + snaps + i) % snaps, slab_of(x, (z_hi + h) % z_hi_n, 1))
 
     with jax.named_scope("b_barrier"):
 
@@ -211,11 +228,11 @@
         def _():
             @pl.when(z_hi < heads)
             def _():
-                pl.semaphore_wait(barrier, snaps - 1 + x_n - 1 + (heads - 1) * len(pairs_at))
+                pl.semaphore_wait(barrier, snaps - 1 + x_n - 1 + (heads - 1) * len(reach))
 
             @pl.when(z_hi >= heads)
             def _():
-                pl.semaphore_wait(barrier, snaps - 1 + x_n - 1 + heads * len(pairs_at))
+                pl.semaphore_wait(barrier, snaps - 1 + x_n - 1 + heads * len(reach))
 
     def part_copy(n, d):
         return remote(
@@ -452,16 +469,17 @@
             sums[pl.ds(snaps - 1, snaps, stride=snaps), :] = jnp.zeros((snaps, SHELLS), jnp.float32)
 
         with jax.named_scope("h_owner"):
-            for d in by_distance:
+            for d in y_steps:
+                yy = (y + d) % y_n
                 remote(
-                    sums.at[rows_of(there(d), snaps)],
-                    r_recv.at[me],
+                    sums.at[rows_of(yy, block)],
+                    r_recv.at[y],
                     r_send,
                     r_rsem,
-                    there(d),
+                    yy * Z_LO + z_lo,
                     slab,
                 ).start()
-            r_recv[me] = sums[rows_of(me, snaps), :]
+            r_recv[y] = sums[rows_of(y, block), :]
             if x_n > 1:
                 arrived(spec_x.at[pl.ds(0, x_n - 1)], t_rsem)
             spec_recv[me] = ordered_sum([spec_x[i] for i in range(x_n)])
@@ -469,8 +487,8 @@
                 remote(
                     spec_recv.at[me], spec_recv.at[me], s_send, s_rsem, there(d), slab
                 ).start()
-            arrived(r_recv.at[pl.ds(0, snaps - 1)], r_rsem)
-            x_recv[x] = ordered_sum([r_recv[t] for t in range(snaps)])
+            arrived(r_recv.at[pl.ds(0, y_n - 1)], r_rsem)
+            x_recv[x] = ordered_sum([r_recv[i] for i in range(y_n)])
 
         with jax.named_scope("i_x"):
             for d in x_steps:
@@ -488,24 +506,41 @@
             arrived(spec_recv.at[pl.ds(0, snaps - 1)], s_rsem)
 
         with jax.named_scope("j_pairs"):
-            own_src[0:snaps, :] = total
             for t in range(snaps):
-                own_src[snaps + t : snaps + t + 1, :] = spec_recv[t]
-            for d in range(1, half + 1):
-                pair_src[d - 1] = total[2 * d - 2 : 2 * d]
+                own_src[t : t + 1, :] = spec_recv[t]
+            for k in range(Z_LO):
+                for d in range(1, half + 1):
+                    row = k * snaps + 2 * d - 2
+                    pair_src[k, d - 1] = total[row : row + 2]
+
+        def pair_copy(h, k, i, send_sem, recv_sem):
+            count = len(pairs_at[i])
+            return remote(
+                pair_src.at[k, pl.ds(pairs_at[i][0] - 1, count)],
+                pair_recv.at[z, slots.index(i), pl.ds(0, count)],
+                send_sem,
+                recv_sem,
+                (base + snaps + k + i) % snaps,
+                slab_of(x, h, 1),
+            )
 
         with jax.named_scope("k_send"):
             for h in range(heads):
-                for i in steps:
-                    count = len(pairs_at[i])
-                    remote(
-                        pair_src.at[pl.ds(pairs_at[i][0] - 1, count)],
-                        pair_recv.at[z_hi, steps.index(i), pl.ds(0, count)],
-                        p_send,
-                        p_rsem,
-                        (me + snaps + i) % snaps,
-                        slab_of(x, h, 1),
-                    ).start()
+                for k, i in away:
+                    pair_copy(h, k, i, p_send, p_rsem).start()
+                for k, i in at_home:
+                    here = (z_hi == h) & (z_lo == k + i)
+
+                    @pl.when(here)
+                    def _(k=k, i=i):
+                        first_pair, count = pairs_at[i][0] - 1, len(pairs_at[i])
+                        pair_recv[z, slots.index(i), 0:count] = pair_src[
+                            k, first_pair : first_pair + count
+                        ]
+
+                    @pl.when(jnp.logical_not(here))
+                    def _(h=h, k=k, i=i):
+                        pair_copy(h, k, i, h_send, h_rsem).start()
 
                 @pl.when(z_hi != h)
                 def _(h=h):
@@ -520,26 +555,22 @@
         @pl.when(z_hi < heads)
         def _():
             with jax.named_scope("l_pairwait"):
-                arrived(many(z_hi_n * pair_rows), p_rsem)
+                arrived(many(z_n * away_rows // Z_LO), p_rsem)
+                arrived(home_rows(z_n - 1), h_rsem)
                 if z_hi_n > 1:
                     arrived(own_recv.at[pl.ds(0, z_hi_n - 1)], o_rsem)
 
             with jax.named_scope("m_coh"):
                 load_order.wait()
                 own = ordered_sum([own_recv[h] for h in range(z_hi_n)])
-                energy = own[snaps : 2 * snaps]
                 for t in range(snaps):
-                    spec_rows[t] = energy[t : t + 1]
+                    spec_rows[t] = own[t : t + 1]
                 spec = spec_rows[me]
                 final[snaps : snaps + 1, :] = spec
 
                 def pair(i, d):
-                    if i == 0:
-                        return own[2 * d - 2 : 2 * d]
                     at = pairs_at[i].index(d)
-                    return ordered_sum(
-                        [pair_recv[h, steps.index(i), at] for h in range(z_hi_n)]
-                    )
+                    return ordered_sum([pair_recv[p, slots.index(i), at] for p in range(z_n)])
 
                 def power(rows):
                     re, im = rows[0:1], rows[1:2]
@@ -581,21 +612,23 @@
         @pl.when(core == 1)
         def _():
             left(src.at[:, pl.ds(0, (snaps - 1) * ROWS)], m_send)
-            left(r_recv.at[pl.ds(0, snaps - 1)], r_send)
+            left(r_recv.at[pl.ds(0, y_n - 1)], r_send)
             if x_n > 1:
                 left(x_recv.at[pl.ds(0, x_n - 1)], x_send)
                 left(spec_x.at[pl.ds(0, x_n - 1)], t_send)
             left(spec_recv.at[pl.ds(0, snaps - 1)], s_send)
-            left(many(heads * pair_rows), p_send)
+            left(many(heads * away_rows), p_send)
 
             @pl.when(z_hi < heads)
             def _():
+                left(home_rows(heads * Z_LO - 1), h_send)
                 if heads > 1:
                     left(own_recv.at[pl.ds(0, heads - 1)], o_send)
                 forwards_left()
 
             @pl.when(z_hi >= heads)
             def _():
+                left(home_rows(heads * Z_LO), h_send)
                 left(own_recv.at[pl.ds(0, heads)], o_send)
 
 
@@ -633,16 +666,16 @@
             pltpu.VMEM((SETS, SHELLS, GROUPS * LANES), bf16),
             pltpu.VMEM(((snaps - 1) * snaps, SHELLS), f32),
             pltpu.VMEM((snaps * snaps, SHELLS), f32),
-            pltpu.VMEM((snaps, snaps, SHELLS), f32),
-            pltpu.VMEM((x_n, snaps, SHELLS), f32),
+            pltpu.VMEM((snaps // Z_LO, Z_LO * snaps, SHELLS), f32),
+            pltpu.VMEM((x_n, Z_LO * snaps, SHELLS), f32),
             pltpu.VMEM((1, SHELLS), f32),
             pltpu.VMEM((1, SHELLS), f32),
             pltpu.VMEM((x_n, 1, SHELLS), f32),
             pltpu.VMEM((snaps, 1, SHELLS), f32),
-            pltpu.VMEM((2 * snaps, SHELLS), f32),
-            pltpu.VMEM((z_hi_n, 2 * snaps, SHELLS), f32),
-            pltpu.VMEM((half, 2, SHELLS), f32),
-            pltpu.VMEM((z_hi_n, half, 2, 2, SHELLS), f32),
+            pltpu.VMEM((snaps, SHELLS), f32),
+            pltpu.VMEM((z_hi_n, snaps, SHELLS), f32),
+            pltpu.VMEM((Z_LO, half, 2, SHELLS), f32),
+            pltpu.VMEM((z_hi_n * Z_LO, half + 1, 2, 2, SHELLS), f32),
             pltpu.VMEM((snaps, 1, SHELLS), f32),
             pltpu.VMEM((snaps, 1, SHELLS), f32),
             pltpu.VMEM((OUT_ROWS, SHELLS), f32),
@@ -651,7 +684,7 @@
             dma((SETS, HALVES)),
             dma(()),
             dma((2,)),
-            *[dma(())] * 16,
+            *[dma(())] * 18,
         ],
         compiler_params=pltpu.CompilerParams(collective_id=0, has_side_effects=True),
     )(vel, ids, ref_order)

time: 36.2 us -> 35.5 us (0.981)
  Pallas kernels: 35.4 us -> 34.8 us
    pallas_call x1, Pallas kernels: 34.8 us -> 34.1 us  [body(): pl.pallas_call(functools.partial(kernel, sizes), out_shape=pltpu.VMEM((sn...]
where the time goes in v6:
time: 35.5 us; the launch traced here: 35.4 us
  Pallas kernels  34.8 us (98%)
  between operations  0.64 us (2%)
    pallas_call x1, Pallas kernels, body(): pl.pallas_call(functools.partial(kernel, sizes), out_shape=pltpu.VMEM((sn...  34.1 us

profile of v6, /device:TPU:1, one launch (start us, length us, event | category | flops | bytes accessed | tf_op | source)
XLA Modules:
  0.0 35.4 jit_solution(16668832107745997808)
XLA Ops:
  0.6 34.1 %shard_map.50.done_ref = f32[17,128]{1,0:T(8,128)S(1)} custom-call(bf16[3,256,128]{2,1,0:T(8,128)(2,1)} %bitcast.6, s32[128,128]{1,0:T(8,128)} %bitcast.7, s32[16]{0:T(128)} %order_hbm.1), custom_call_target="tpu_custom_call" | custom-call | tf_op jit(solution)/shard_map/pallas_call | solution.py:653
  34.8 0.6 %shard_map.51 = (f32[1,16,128]{2,1,0:T(8,128)}, f32[1,128]{1,0:T(1,128)}) custom-call(f32[17,128]{1,0:T(8,128)S(1)} %shard_map.50.done_ref), custom_call_target="tpu_custom_call" | custom-call | tf_op jit(solution)/shard_map/pallas_call | solution.py:691

commit v7 on v6

--- a/solution.py
+++ b/solution.py
@@ -116,6 +116,7 @@
     is_late = z_hi // heads
     part_set = core + (1 - core) * 2 * is_late
     by_distance = sorted(range(1, snaps), key=lambda d: (-min(d, snaps - d), d))
+    far_ones, near_ones = by_distance[: half - 1], by_distance[half - 1 :]
 
     pairs_at = {0: (1,)}
     for step in range(1, (half + 1) // 2 + 1):
@@ -343,9 +344,10 @@
 
     @pl.when(core == 0)
     def _():
-        for n in range(HALVES):
-            for d in [*by_distance, 0]:
-                part_copy(n, d).start()
+        for some in (far_ones, [*near_ones, 0]):
+            for n in range(HALVES):
+                for d in some:
+                    part_copy(n, d).start()
         load_ids.wait()
         ids_copy().start()
         spec_out[...] = local_spectrum()
@@ -353,9 +355,10 @@
 
     @pl.when(core == 1)
     def _():
-        for n in range(HALVES):
-            for d in by_distance:
-                part_copy(n, d).start()
+        for some in (far_ones, near_ones):
+            for n in range(HALVES):
+                for d in some:
+                    part_copy(n, d).start()
 
         first = lax.broadcasted_iota(jnp.int32, (snaps, LANES), 0) < half
 

time: 35.5 us -> 35.2 us (level)
  Pallas kernels: 34.8 us -> 34.4 us
where the time goes in v7:
time: 35.2 us; the launch traced here: 35.1 us
  Pallas kernels  34.4 us (98%)
  between operations  0.64 us (2%)
    pallas_call x1, Pallas kernels, body(): pl.pallas_call(functools.partial(kernel, sizes), out_shape=pltpu.VMEM((sn...  33.8 us

profile of v7, /device:TPU:1, one launch (start us, length us, event | category | flops | bytes accessed | tf_op | source)
XLA Modules:
  0.0 35.1 jit_solution(6264264742490243624)
XLA Ops:
  0.6 33.8 %shard_map.50.done_ref = f32[17,128]{1,0:T(8,128)S(1)} custom-call(bf16[3,256,128]{2,1,0:T(8,128)(2,1)} %bitcast.6, s32[128,128]{1,0:T(8,128)} %bitcast.7, s32[16]{0:T(128)} %order_hbm.1), custom_call_target="tpu_custom_call" | custom-call | tf_op jit(solution)/shard_map/pallas_call | solution.py:656
  34.5 0.6 %shard_map.51 = (f32[1,16,128]{2,1,0:T(8,128)}, f32[1,128]{1,0:T(1,128)}) custom-call(f32[17,128]{1,0:T(8,128)S(1)} %shard_map.50.done_ref), custom_call_target="tpu_custom_call" | custom-call | tf_op jit(solution)/shard_map/pallas_call | solution.py:694

commit v8 on v7

--- a/solution.py
+++ b/solution.py
@@ -72,6 +72,7 @@
     pair_src,
     pair_recv,
     spec_rows,
+    power_rows,
     coh_rows,
     final,
     load_sem,
@@ -116,7 +117,7 @@
     is_late = z_hi // heads
     part_set = core + (1 - core) * 2 * is_late
     by_distance = sorted(range(1, snaps), key=lambda d: (-min(d, snaps - d), d))
-    far_ones, near_ones = by_distance[: half - 1], by_distance[half - 1 :]
+    far_ones, near_ones = by_distance[: half - 2], by_distance[half - 2 :]
 
     pairs_at = {0: (1,)}
     for step in range(1, (half + 1) // 2 + 1):
@@ -503,14 +504,26 @@
                     me,
                     slab_of((x + d) % x_n, z_hi, 1),
                 ).start()
+            arrived(spec_recv.at[pl.ds(0, snaps - 1)], s_rsem)
+            for t in range(snaps):
+                own_src[t : t + 1, :] = spec_recv[t]
+            for h in range(heads):
+
+                @pl.when(z_hi != h)
+                def _(h=h):
+                    remote(
+                        own_src, own_recv.at[z_hi], o_send, o_rsem, me, slab_of(x, h, 1)
+                    ).start()
+
+                @pl.when(z_hi == h)
+                def _(h=h):
+                    own_recv[h] = own_src[...]
+
             if x_n > 1:
                 arrived(x_recv.at[pl.ds(0, x_n - 1)], x_rsem)
             total = ordered_sum([x_recv[i] for i in range(x_n)])
-            arrived(spec_recv.at[pl.ds(0, snaps - 1)], s_rsem)
 
         with jax.named_scope("j_pairs"):
-            for t in range(snaps):
-                own_src[t : t + 1, :] = spec_recv[t]
             for k in range(Z_LO):
                 for d in range(1, half + 1):
                     row = k * snaps + 2 * d - 2
@@ -545,15 +558,12 @@
                     def _(h=h, k=k, i=i):
                         pair_copy(h, k, i, h_send, h_rsem).start()
 
-                @pl.when(z_hi != h)
-                def _(h=h):
-                    remote(
-                        own_src, own_recv.at[z_hi], o_send, o_rsem, me, slab_of(x, h, 1)
-                    ).start()
-
-                @pl.when(z_hi == h)
-                def _(h=h):
-                    own_recv[h] = own_src[...]
+        left(src.at[:, pl.ds(0, (snaps - 1) * ROWS)], m_send)
+        left(r_recv.at[pl.ds(0, y_n - 1)], r_send)
+        if x_n > 1:
+            left(x_recv.at[pl.ds(0, x_n - 1)], x_send)
+            left(spec_x.at[pl.ds(0, x_n - 1)], t_send)
+        left(spec_recv.at[pl.ds(0, snaps - 1)], s_send)
 
         @pl.when(z_hi < heads)
         def _():
@@ -566,9 +576,8 @@
             with jax.named_scope("m_coh"):
                 load_order.wait()
                 own = ordered_sum([own_recv[h] for h in range(z_hi_n)])
-                for t in range(snaps):
-                    spec_rows[t] = own[t : t + 1]
-                spec = spec_rows[me]
+                spec_rows[...] = own
+                spec = spec_rows[pl.ds(me, 1), :]
                 final[snaps : snaps + 1, :] = spec
 
                 def pair(i, d):
@@ -580,7 +589,7 @@
                     return re * re + im * im
 
                 def put_row(e, value):
-                    coh_rows[e] = value / (spec * spec_rows[(me + snaps - e) % snaps])
+                    power_rows[pl.ds((me + snaps - e) % snaps, 1), :] = value
 
                 put_row(0, spec * spec)
                 for d in range(1, half):
@@ -589,8 +598,9 @@
                 re = pair((half + 1) // 2, half)[0:1]
                 im = pair(-(half // 2), half)[0:1]
                 put_row(half, re * re + im * im)
+                coh_rows[...] = power_rows[...] / (spec * own)
                 for j in range(snaps):
-                    final[j : j + 1, :] = coh_rows[(me - order_ref[j] + snaps) % snaps]
+                    final[j : j + 1, :] = coh_rows[pl.ds(order_ref[j], 1), :]
                 forward_all()
 
         @pl.when(z_hi >= heads)
@@ -614,12 +624,6 @@
 
         @pl.when(core == 1)
         def _():
-            left(src.at[:, pl.ds(0, (snaps - 1) * ROWS)], m_send)
-            left(r_recv.at[pl.ds(0, y_n - 1)], r_send)
-            if x_n > 1:
-                left(x_recv.at[pl.ds(0, x_n - 1)], x_send)
-                left(spec_x.at[pl.ds(0, x_n - 1)], t_send)
-            left(spec_recv.at[pl.ds(0, snaps - 1)], s_send)
             left(many(heads * away_rows), p_send)
 
             @pl.when(z_hi < heads)
@@ -679,8 +683,9 @@
             pltpu.VMEM((z_hi_n, snaps, SHELLS), f32),
             pltpu.VMEM((Z_LO, half, 2, SHELLS), f32),
             pltpu.VMEM((z_hi_n * Z_LO, half + 1, 2, 2, SHELLS), f32),
-            pltpu.VMEM((snaps, 1, SHELLS), f32),
-            pltpu.VMEM((snaps, 1, SHELLS), f32),
+            pltpu.VMEM((snaps, SHELLS), f32),
+            pltpu.VMEM((snaps, SHELLS), f32),
+            pltpu.VMEM((snaps, SHELLS), f32),
             pltpu.VMEM((OUT_ROWS, SHELLS), f32),
             dma((3,)),
             dma(()),

time: 35.2 us -> 35.1 us (level)
  no operation moved by 1% of the time
where the time goes in v8:
time: 35.1 us; the launch traced here: 35 us
  Pallas kernels  34.3 us (98%)
  between operations  0.64 us (2%)
    pallas_call x1, Pallas kernels, body(): pl.pallas_call(functools.partial(kernel, sizes), out_shape=pltpu.VMEM((sn...  33.7 us

profile of v8, /device:TPU:1, one launch (start us, length us, event | category | flops | bytes accessed | tf_op | source)
XLA Modules:
  0.0 35.0 jit_solution(1275505508315107953)
XLA Ops:
  0.6 33.7 %shard_map.50.done_ref = f32[17,128]{1,0:T(8,128)S(1)} custom-call(bf16[3,256,128]{2,1,0:T(8,128)(2,1)} %bitcast.6, s32[128,128]{1,0:T(8,128)} %bitcast.7, s32[16]{0:T(128)} %order_hbm.1), custom_call_target="tpu_custom_call" | custom-call | tf_op jit(solution)/shard_map/pallas_call | solution.py:660
  34.4 0.6 %shard_map.51 = (f32[1,16,128]{2,1,0:T(8,128)}, f32[1,128]{1,0:T(1,128)}) custom-call(f32[17,128]{1,0:T(8,128)S(1)} %shard_map.50.done_ref), custom_call_target="tpu_custom_call" | custom-call | tf_op jit(solution)/shard_map/pallas_call | solution.py:699

commit v9 on v8

--- a/solution.py
+++ b/solution.py
@@ -495,15 +495,14 @@
             x_recv[x] = ordered_sum([r_recv[i] for i in range(y_n)])
 
         with jax.named_scope("i_x"):
-            for d in x_steps:
-                remote(
-                    x_recv.at[x],
-                    x_recv.at[x],
-                    x_send,
-                    x_rsem,
-                    me,
-                    slab_of((x + d) % x_n, z_hi, 1),
-                ).start()
+            for xx in range(x_n):
+
+                @pl.when(x != xx)
+                def _(xx=xx):
+                    remote(
+                        x_recv.at[x], x_recv.at[x], x_send, x_rsem, me, slab_of(xx, z_hi, 1)
+                    ).start()
+
             arrived(spec_recv.at[pl.ds(0, snaps - 1)], s_rsem)
             for t in range(snaps):
                 own_src[t : t + 1, :] = spec_recv[t]

time: 35.1 us -> 35.1 us (level)
  no operation moved by 1% of the time
where the time goes in v9:
time: 35.1 us; the launch traced here: 35 us
  Pallas kernels  34.4 us (98%)
  between operations  0.64 us (2%)
    pallas_call x1, Pallas kernels, body(): pl.pallas_call(functools.partial(kernel, sizes), out_shape=pltpu.VMEM((sn...  33.7 us

profile of v9, /device:TPU:1, one launch (start us, length us, event | category | flops | bytes accessed | tf_op | source)
XLA Modules:
  0.0 35.0 jit_solution(6945867424494948627)
XLA Ops:
  0.6 33.7 %shard_map.50.done_ref = f32[17,128]{1,0:T(8,128)S(1)} custom-call(bf16[3,256,128]{2,1,0:T(8,128)(2,1)} %bitcast.6, s32[128,128]{1,0:T(8,128)} %bitcast.7, s32[16]{0:T(128)} %order_hbm.1), custom_call_target="tpu_custom_call" | custom-call | tf_op jit(solution)/shard_map/pallas_call | solution.py:659
  34.4 0.6 %shard_map.51 = (f32[1,16,128]{2,1,0:T(8,128)}, f32[1,128]{1,0:T(1,128)}) custom-call(f32[17,128]{1,0:T(8,128)S(1)} %shard_map.50.done_ref), custom_call_target="tpu_custom_call" | custom-call | tf_op jit(solution)/shard_map/pallas_call | solution.py:698
